TPU v7x, 128 devices: a whole 4x4x4 slice. The times are simulated.
128 devices in a mesh: row: 2 (over x_lo), col: 64 (over z, y, x_hi, core).
Axes of the slice: x: 4 (x_hi: 2, x_lo: 2; x = x_hi * 2 + x_lo), y: 4, z: 4, core: 2. Of those that a mesh axis runs over, the one named last changes fastest.
Arguments:
- panel: bfloat16 [196608, 1024], P('col', 'row'), may hold values from -0.1875 to 0.1875
- rhs: float32 [1024, 196608], P('row', 'col'), may hold values from -6 to 6
- diag_inverse: bfloat16 [2, 512, 512], replicated, may hold values from -1 to 2, as said below
Outputs:
- solved: bfloat16 [1024, 1024], P(None, 'row')
- updated: float32 [1024, 196608], P('row', 'col')
Inputs may be any that keep to these rules, and one draw needn't show every extreme that they name: `diag_inverse`: each block is lower triangular; its diagonal entries are 0.5 or more.
All inputs are finite; a program needn't handle non-finite values.
Results may differ from a plain program's by a relative error of at most 0.0065.
Values may be sent and summed in bfloat16 or wider, within the bound.
No kernel may reach another device: no remote copies, remote signals or barrier semaphores. Data moves between devices by JAX's collectives and lax.ppermute only.
A program may use at most 128 MiB of HBM per device.

v0:
```python
import jax
import jax.numpy as jnp
from jax import lax
from jax.sharding import PartitionSpec as P


def rows_for(lines, length):
    spare = -len(lines) % length
    return jnp.pad(lines, [(0, spare)] + [(0, 0)] * (lines.ndim - 1))


def broadcast_by_parts(value, axis, root):
    lines = jnp.where(lax.axis_index(axis) == root, value, jnp.zeros_like(value)).reshape(
        -1, *value.shape[1:][-1:]
    )
    padded = rows_for(lines, lax.axis_size(axis))
    own = lax.psum_scatter(padded, axis, scatter_dimension=0, tiled=True)
    return lax.all_gather(own, axis, axis=0, tiled=True)[: len(lines)].reshape(value.shape)


def from_everyone(value, axis):
    copies = jnp.broadcast_to(value, (lax.axis_size(axis), *value.shape))
    return lax.all_to_all(copies, axis, split_axis=0, concat_axis=0, tiled=True)


def taken_together(value, axis):
    return from_everyone(value, axis).sum(axis=0)


def split_up(value, dim, length):
    lengths = value.shape
    tiles = value.reshape(*lengths[:dim], length, lengths[dim] // length, *lengths[dim + 1 :])
    return jnp.moveaxis(tiles, dim, 0)


def sum_at_owner(value, axis, dim):
    tiles = split_up(value, dim, lax.axis_size(axis))
    arrived = lax.all_to_all(tiles, axis, split_axis=0, concat_axis=0, tiled=True)
    return arrived.astype(jnp.float32).sum(axis=0)


def spread_block(values, owner):
    return broadcast_by_parts(values, "col", owner)


def shards(panel, rhs, diag_inverse):
    block_size = diag_inverse.shape[1]
    step_count = diag_inverse.shape[0]
    rows_dev = panel.shape[0]
    slice_count = rhs.shape[0]
    rhs_count = slice_count * lax.axis_size("row")
    row_index = lax.axis_index("row")
    col_index = lax.axis_index("col")
    dropped = (col_index < step_count) & (row_index >= col_index)
    top_block = jnp.where(dropped, jnp.zeros_like(panel[:block_size]), panel[:block_size])
    masked = jnp.concatenate([top_block, panel[block_size:]], axis=0)
    contract = (((1,), (1,)), ((), ()))
    own_solved = jnp.zeros((rhs_count, block_size), jnp.bfloat16)
    products = jnp.zeros((rhs_count, rows_dev), jnp.float32)
    for current in range(step_count):
        inverse = diag_inverse[current].astype(jnp.float32)
        partial_value = lax.cond(
            col_index == current,
            lambda: lax.dot_general(
                own_solved, masked[:block_size], contract, preferred_element_type=jnp.float32
            ),
            lambda: jnp.zeros((rhs_count, block_size), jnp.float32),
        )
        embedded = lax.dynamic_update_slice(
            jnp.zeros((rhs_count, block_size), jnp.float32),
            rhs[:, :block_size],
            (row_index * slice_count, jnp.int32(0)),
        )
        residual = taken_together(embedded - partial_value, "row")
        whole_block = jnp.dot(residual, inverse.T, precision=lax.Precision.HIGHEST).astype(
            jnp.bfloat16
        )
        arrived = spread_block(whole_block, current)
        own_solved = jnp.where(row_index == current, arrived, own_solved)
        products = lax.cond(
            row_index == current,
            lambda: lax.dot_general(arrived, masked, contract, preferred_element_type=jnp.float32),
            lambda: products,
        )
    reduced = sum_at_owner(products.astype(jnp.bfloat16), "row", 0)
    updated = rhs - reduced
    return (own_solved, updated)


def solution(mesh):
    placed = (P("col", "row"), P("row", "col"), P())
    return jax.shard_map(
        shards,
        mesh=mesh,
        in_specs=placed,
        out_specs=(P(None, "row"), P("row", "col")),
        check_vma=False,
    )
```

profile of v0, /device:TPU:1, one launch (start us, length us, event | category | flops | bytes accessed | tf_op | source)
XLA Modules:
  0.0 1041.3 jit_solution(9920857579655382945)
XLA Ops:
  7.2 1.1 slice_select_fusion
  8.3 0.2 broadcast.15
  8.6 1.3 slice_dynamic-update-slice_fusion
  9.9 1.6 conditional.4
  9.9 1.6 broadcast.10
  11.5 2.1 sub.9
  13.5 0.6 broadcast_in_dim.13
  14.1 50.4 %all_to_all.15 = f32[2,1024,512]{2,1,0:T(8,128)} all-to-all(f32[2,1024,512]{2,1,0:T(8,128)S(1)} %broadcast_in_dim.13), channel_id=1, replica_groups=mesh['row'=2,'col'=64] {'row'}, dimensions={0} | all-to-all | bytes 8388608 | tf_op jit(solution)/shard_map/all_to_all | solution.py:23
  64.6 4.2 reduce_sum.27
  68.7 4.5 fusion.3
  73.2 0.0 all-gather.3.cloned.1.call-start
  73.3 334.0 %reduce-scatter.3.cloned.1.call-done = bf16[16,512]{1,0:T(8,128)(2,1)} async-done(((bf16[1024,512]{1,0:T(8,128)(2,1)}), bf16[16,512]{1,0:T(8,128)(2,1)}) %reduce-scatter.3.cloned.1.call-update) | async-done | bytes 16400 | tf_op jit(solution)/shard_map/reduce_scatter | solution.py:17
  407.4 70.8 %all-gather.3.cloned.1.call-done = bf16[1024,512]{1,0:T(8,128)(2,1)} async-done(((bf16[16,512]{1,0:T(8,128)(2,1)}), bf16[1024,512]{1,0:T(8,128)(2,1)}) %all-gather.3.cloned.1.call-update) | async-done | bytes 1048592 | tf_op jit(solution)/shard_map/all_gather | solution.py:18
  478.1 2.3 broadcast_select_fusion
  480.4 3.3 conditional.5
  480.4 3.3 fusion.9
  483.7 2.1 sub.10
  485.8 0.6 broadcast_in_dim.14
  486.4 50.4 %all_to_all.16 = f32[2,1024,512]{2,1,0:T(8,128)} all-to-all(f32[2,1024,512]{2,1,0:T(8,128)S(1)} %broadcast_in_dim.14), channel_id=1, replica_groups=mesh['row'=2,'col'=64] {'row'}, dimensions={0} | all-to-all | bytes 8388608 | tf_op jit(solution)/shard_map/all_to_all | solution.py:23
  536.7 2.9 reduce_sum.28
  539.6 3.9 fusion.4
  543.5 0.0 all-gather.5.cloned.1.call-start
  543.5 325.5 %reduce-scatter.5.cloned.1.call-done = bf16[16,512]{1,0:T(8,128)(2,1)} async-done(((bf16[1024,512]{1,0:T(8,128)(2,1)}), bf16[16,512]{1,0:T(8,128)(2,1)}) %reduce-scatter.5.cloned.1.call-update) | async-done | bytes 16400 | tf_op jit(solution)/shard_map/reduce_scatter | solution.py:17
  869.1 1.8 pad_maximum_fusion
  870.9 8.4 conditional.6
  870.9 8.4 fusion.10
  879.3 60.2 %all-gather.5.cloned.1.call-done = bf16[1024,512]{1,0:T(8,128)(2,1)} async-done(((bf16[16,512]{1,0:T(8,128)(2,1)}), bf16[1024,512]{1,0:T(8,128)(2,1)}) %all-gather.5.cloned.1.call-update) | async-done | bytes 1048592 | tf_op jit(solution)/shard_map/all_gather | solution.py:18
  939.5 10.1 all-to-all-start.2
  949.6 1.1 broadcast_select_fusion.1
  950.7 72.5 %all-to-all-done.2 = bf16[2,512,3072]{2,1,0:T(8,128)(2,1)} async-done(((bf16[2,512,3072]{2,1,0:T(8,128)(2,1)}), bf16[2,512,3072]{2,1,0:T(8,128)(2,1)}, u32[]{:S(2)}, u32[]{:S(2)}) %all-to-all-start.2) | async-done | bytes 6291488 | tf_op jit(solution)/shard_map/all_to_all | solution.py:38
  1023.1 5.0 convert_reduce_fusion
  1028.1 6.6 sub.11
  (13 shorter events, 0.2 us)
Async XLA Ops:
  7.2 400.1 %reduce-scatter.3.cloned.1.call-start = ((), (), s32[]{:S(2)}) async-start(), calls=%async_computation.5 | async-start | bytes 1064960 | tf_op jit(solution)/shard_map/reduce_scatter | solution.py:17
  73.2 404.9 %all-gather.3.cloned.1.call-start = ((), (), s32[]{:S(2)}) async-start(), calls=%async_computation.6 | async-start | bytes 1064960 | tf_op jit(solution)/shard_map/all_gather | solution.py:18
  407.3 461.7 %reduce-scatter.5.cloned.1.call-start = ((), (), s32[]{:S(2)}) async-start(), calls=%async_computation.7 | async-start | bytes 1064960 | tf_op jit(solution)/shard_map/reduce_scatter | solution.py:17
  543.4 325.6 %slice-start = ((bf16[3072,512]{1,0:T(8,128)(2,1)}), bf16[2560,512]{1,0:T(8,128)(2,1)S(1)}, s32[]{:S(2)}) async-start(bf16[3072,512]{1,0:T(8,128)(2,1)} %param.11), calls=%async_computation.9 | async-start | bytes 5242880 | tf_op jit(solution)/shard_map/slice | solution.py:56
  543.5 396.0 %all-gather.5.cloned.1.call-start = ((), (), s32[]{:S(2)}) async-start(), calls=%async_computation.8 | async-start | bytes 1064960 | tf_op jit(solution)/shard_map/all_gather | solution.py:18
  939.5 10.1 copy-start
  939.5 10.1 copy-start.1
  939.5 83.6 %all-to-all-start.2 = ((bf16[2,512,3072]{2,1,0:T(8,128)(2,1)}), bf16[2,512,3072]{2,1,0:T(8,128)(2,1)}, u32[]{:S(2)}, u32[]{:S(2)}) async-start(bf16[2,512,3072]{2,1,0:T(8,128)(2,1)} %bitcast.16), calls=%async_computation.4 | async-start | bytes 12582912 | tf_op jit(solution)/shard_map/all_to_all | solution.py:38
Sparse Core Ops, SparseCore 0:
  73.3 333.9 reduce-scatter.2
  410.5 67.5 all-gather.2
  543.6 325.4 reduce-scatter.4
  872.1 67.3 all-gather.4
where the time goes:
time: 1040 us
  waiting for transfers between devices  863 us (83%)
  blocking collectives  101 us (10%)
  other arithmetic  29 us (3%)
  matrix products  20 us (2%)
  between operations  13.8 us (1%)
    reduce_scatter x2, waiting for transfers between devices, broadcast_by_parts(): own = lax.psum_scatter(padded, axis, scatter_dimension=0, tiled=True)  660 us
    all_gather x2, waiting for transfers between devices, broadcast_by_parts(): lax.all_gather(own, axis, axis=0, tiled=True)[:len(lines)]  131 us
    all_to_all x2, blocking collectives, from_everyone(): return lax.all_to_all(copies, axis, split_axis=0, concat_axis=0, tiled=True)  101 us
    all_to_all x1, waiting for transfers between devices, sum_at_owner(): lax.all_to_all(tiles, axis, split_axis=0, concat_axis=0, tiled=True)  72.5 us
  transfers between devices with their start and end apart: 5, of which 5 were waited for; matrix products, arithmetic and copies ran while one was open for 1% of the time, Pallas kernels for 0%

commit v1 on v0

v1 whole, which is shorter than its diff:
```python
import functools

import jax
import jax.numpy as jnp
from jax import lax
from jax.experimental import pallas as pl
from jax.experimental.pallas import tpu as pltpu
from jax.sharding import Mesh
from jax.sharding import PartitionSpec as P


NB = 512
COL = ("z", "y", "xh", "core")
ALL = ("row",) + COL
NT = (((1,), (1,)), ((), ()))
F32 = jnp.float32
BF16 = jnp.bfloat16
CUTS = (0, 512, 1024, 1536, 2048, 2560, 3072)
TILE = 256
PARAMS = pltpu.CompilerParams(vmem_limit_bytes=16 << 20)


def dot_nt(a, b):
    return lax.dot_general(a, b, NT, preferred_element_type=F32)


def times_inverse(x, inverse):
    high = x.astype(BF16)
    rest = x - high.astype(F32)
    mid = rest.astype(BF16)
    low = (rest - mid.astype(F32)).astype(BF16)
    return dot_nt(low, inverse) + dot_nt(mid, inverse) + dot_nt(high, inverse)


def first_body(rhs_ref, inv_ref, out_ref):
    out_ref[...] = times_inverse(rhs_ref[...], inv_ref[0]).astype(BF16)


def first_solve(rhs, diag_inverse):
    step = NB // 2
    return pl.pallas_call(
        first_body,
        grid=(2,),
        in_specs=[
            pl.BlockSpec((step, NB), lambda i: (i, 0)),
            pl.BlockSpec((1, NB, NB), lambda i: (0, 0, 0)),
        ],
        out_specs=pl.BlockSpec((step, NB), lambda i: (i, 0)),
        out_shape=jax.ShapeDtypeStruct((NB, NB), BF16),
        compiler_params=PARAMS,
        cost_estimate=pl.CostEstimate(flops=6 * NB**3, bytes_accessed=4 << 20, transcendentals=0),
        name="first_solve",
    )(rhs, diag_inverse)


def second_body(flags, rhs_ref, inv_ref, own_ref, arrived_ref, below_ref, sent_ref, *outs):
    below = jnp.where(flags[0] == 0, below_ref[...], sent_ref[...])
    part = NB // len(outs)
    for q, out in enumerate(outs):
        rows = pl.ds(q * part, part)
        residual = rhs_ref[rows, :] - dot_nt(arrived_ref[rows, :], below)
        second = times_inverse(residual, inv_ref[0]).astype(BF16)
        out[...] = jnp.where(flags[1] == 0, own_ref[rows, :], second)


def second_solve(flags, rhs, diag_inverse, own, arrived, panel, sent):
    whole = pl.BlockSpec((NB, NB), lambda i, f: (0, 0))
    part = pl.BlockSpec((NB // 4, NB), lambda i, f: (0, 0))
    return pl.pallas_call(
        second_body,
        grid_spec=pltpu.PrefetchScalarGridSpec(
            num_scalar_prefetch=1,
            grid=(1,),
            in_specs=[whole, pl.BlockSpec((1, NB, NB), lambda i, f: (1, 0, 0))] + [whole] * 4,
            out_specs=[part] * 4,
        ),
        out_shape=[jax.ShapeDtypeStruct((NB // 4, NB), BF16)] * 4,
        compiler_params=PARAMS,
        cost_estimate=pl.CostEstimate(flops=8 * NB**3, bytes_accessed=4 << 20, transcendentals=0),
        name="second_solve",
    )(flags, rhs, diag_inverse, own, arrived, panel, sent)


def vmem_call(body, flags, operands, outs):
    return pl.pallas_call(
        body,
        in_specs=[pl.BlockSpec(memory_space=pltpu.SMEM)]
        + [pl.BlockSpec(memory_space=pltpu.VMEM)] * len(operands),
        out_specs=[pl.BlockSpec(memory_space=pltpu.VMEM)] * len(outs),
        out_shape=[jax.ShapeDtypeStruct(shape, BF16) for shape in outs],
        compiler_params=PARAMS,
        cost_estimate=pl.CostEstimate(flops=1 << 20, bytes_accessed=1 << 20, transcendentals=0),
    )(flags, *operands)


def ring_body(flags, own, up, down, far, out):
    y = flags[3]
    out[y] = own[...]
    out[lax.rem(y + 1, 4)] = down[...]
    out[lax.rem(y + 2, 4)] = far[...]
    out[lax.rem(y + 3, 4)] = up[...]


def plane_body(flags, own, up, down, far_a, far_b, out):
    z = flags[2]
    for y in range(4):
        rows = slice(y * 32, y * 32 + 32)
        far = far_a if y < 2 else far_b
        for h in range(2):
            out[h, z, rows] = own[y, h]
            out[h, lax.rem(z + 1, 4), rows] = down[y, h]
            out[h, lax.rem(z + 2, 4), rows] = far[y % 2, h]
            out[h, lax.rem(z + 3, 4), rows] = up[y, h]


def finish_body(flags, mine, theirs, solved, left, right):
    row = flags[0]
    same = flags[1] == row
    for h in range(2):
        rows = pl.ds(h * NB, NB)
        solved[rows, :] = jnp.where(same, mine[h], theirs[h])
    left[...] = jnp.where(same, mine[row], theirs[row])
    right[...] = jnp.where(same, theirs[row], mine[row])


def update_body(masks, flags, left, right, rhs, own, other, *rest):
    out = rest[-1]
    first = dot_nt(left[...], own[...])
    if masks:
        arrived = jnp.where(flags[6] == 0, other[...], rest[0][...])
        second = dot_nt(right[...], arrived)
        first = jnp.where(flags[4] == 0, jnp.zeros_like(first), first)
        second = jnp.where(flags[5] == 0, jnp.zeros_like(second), second)
    else:
        second = dot_nt(right[...], other[...])
    out[...] = rhs[...] - (first + second)


def update(flags, left, right, rhs, panel, other, start, stop, before, sent):
    base = start // TILE
    whole = pl.BlockSpec((NB, NB), lambda i, f: (0, 0))
    across = pl.BlockSpec((NB, TILE), lambda i, f: (0, base + i))
    arrived = pl.BlockSpec((TILE, NB), lambda i, f: (i, 0))
    operands = [left, right, rhs, panel, other]
    specs = [whole, whole, across, pl.BlockSpec((TILE, NB), lambda i, f: (base + i, 0)), arrived]
    aliases = {}
    if sent is not None:
        operands.append(sent)
        specs.append(arrived)
    if before is not None:
        aliases = {1 + len(operands): 0}
        operands.append(before)
        specs.append(pl.BlockSpec(memory_space=pl.ANY))
    return pl.pallas_call(
        functools.partial(update_body, sent is not None),
        grid_spec=pltpu.PrefetchScalarGridSpec(
            num_scalar_prefetch=1,
            grid=((stop - start) // TILE,),
            in_specs=specs,
            out_specs=across,
        ),
        out_shape=jax.ShapeDtypeStruct(rhs.shape, F32),
        input_output_aliases=aliases,
        compiler_params=PARAMS,
        cost_estimate=pl.CostEstimate(
            flops=4 * NB * NB * (stop - start), bytes_accessed=4 << 20, transcendentals=0
        ),
        name="update",
    )(flags, *operands)


def shards(panel, rhs, diag_inverse):
    row, z, y, xh, core = (lax.axis_index(name) for name in ALL)
    col = ((z * 4 + y) * 2 + xh) * 2 + core
    window = col < 2
    keep_own = jnp.logical_not(window & (row >= col))
    keep_other = jnp.logical_not(window & (1 - row >= col))
    flags = jnp.stack(
        [a.astype(jnp.int32) for a in (row, core, z, y, keep_own, keep_other, window)]
    )
    swap = [(0, 1), (1, 0)]
    pieces = [panel[a:b] for a, b in zip(CUTS[:-1], CUTS[1:])]

    def shift(value, axis, by):
        return lax.ppermute(value, axis, [(i, (i + by) % 4) for i in range(4)])

    sent = lax.ppermute(pieces[0], ALL, [(1, 65)])
    pairs = [(c, 64 + c) for c in range(2, 64)]
    others = [lax.ppermute(pieces[0], ALL, pairs + [(b, a) for a, b in pairs])]
    for k in range(1, len(pieces)):
        others.append(lax.ppermute(pieces[k], "row", swap))
    first = first_solve(rhs, diag_inverse)
    arrived = lax.ppermute(first, "core", [(0, 1)])
    quarters = second_solve(flags, rhs, diag_inverse, first, arrived, panel, sent)

    got = [lax.ppermute(quarters[q], "z", [(0, q)]) for q in range(1, 4)]
    mine = jnp.where(
        z == 0, quarters[0], jnp.where(z == 1, got[0], jnp.where(z == 2, got[1], got[2]))
    )
    got = [lax.ppermute(mine[32 * q : 32 * q + 32], "y", [(0, q)]) for q in range(1, 4)]
    mine = jnp.where(y == 0, mine[:32], jnp.where(y == 1, got[0], jnp.where(y == 2, got[1], got[2])))
    theirs = lax.ppermute(mine, "row", swap)
    both = jnp.stack([jnp.where(row == 0, mine, theirs), jnp.where(row == 0, theirs, mine)])
    over = lax.ppermute(both, ("row", "xh"), [(2, 1), (0, 3)])
    both = jnp.where(xh == 0, both, over)
    up, down, far = (shift(both, "y", by) for by in (1, -1, 2))
    (line,) = vmem_call(ring_body, flags, [both, up, down, far], [(4, 2, 32, NB)])
    up, down = shift(line, "z", 1), shift(line, "z", -1)
    far_a, far_b = shift(up[:2], "z", 1), shift(down[2:], "z", -1)
    (plane,) = vmem_call(plane_body, flags, [line, up, down, far_a, far_b], [(2, 4, 128, NB)])
    plane = plane.reshape(2, NB, NB)
    theirs = lax.ppermute(plane, "core", swap)
    solved, left, right = vmem_call(
        finish_body, flags, [plane, theirs], [(2 * NB, NB), (NB, NB), (NB, NB)]
    )
    updated = None
    for k, other in enumerate(others):
        updated = update(
            flags, left, right, rhs, panel, other, CUTS[k], CUTS[k + 1], updated,
            sent if k == 0 else None,
        )
    return solved, updated


def solution(mesh):
    split = Mesh(mesh.devices.reshape(2, 4, 4, 2, 2), ALL)
    return jax.shard_map(
        shards,
        mesh=split,
        in_specs=(P(COL, "row"), P("row", COL), P()),
        out_specs=(P(None, "row"), P("row", COL)),
        check_vma=False,
    )
```

time: 1040 us -> 160 us (0.15)
  the two profiles are of different devices: /device:TPU:1 before, /device:TPU:6 now
where the time goes in v1:
time: 160 us; the launch traced here: 159 us
  waiting for transfers between devices  75.1 us (47%)
  starting transfers between devices  44.3 us (28%)
  Pallas kernels  25.7 us (16%)
  local copies, waits for them, and re-layouts  12.6 us (8%)
    ppermute x5, waiting for transfers between devices, shards(): others.append(lax.ppermute(pieces[k], 'row', swap))  36.2 us
    ppermute x7, waiting for transfers between devices, shift(): return lax.ppermute(value, axis, [(i, (i + by) % 4) for i in range(4)])  15.5 us
    pallas_call x6, Pallas kernels, update(): pl.pallas_call(functools.partial(update_body, sent is not None), grid_spe...  15.4 us
    ppermute x7, starting transfers between devices, shift(): return lax.ppermute(value, axis, [(i, (i + by) % 4) for i in range(4)])  12.7 us
    ppermute x1, waiting for transfers between devices, shards(): others = [lax.ppermute(pieces[0], ALL, pairs + [(b, a) for a, b in pairs])]  10.9 us
    unnamed x12, local copies, waits for them, and re-layouts  10.8 us
    ppermute x3, starting transfers between devices, shards(): got = [lax.ppermute(quarters[q], 'z', [(0, q)]) for q in range(1, 4)]  9.69 us
    ppermute x3, starting transfers between devices, shards(): lax.ppermute(mine[32 * q:32 * q + 32], 'y', [(0, q)])  7.5 us
  transfers between devices with their start and end apart: 24, of which 17 were waited for; matrix products, arithmetic and copies ran while one was open for 1% of the time, Pallas kernels for 9%

profile of v1, /device:TPU:6, one launch (start us, length us, event | category | flops | bytes accessed | tf_op | source)
XLA Modules:
  0.0 159.5 jit_solution(15254271911839318525)
XLA Ops:
  0.6 2.8 %copy-done = f32[512,3072]{1,0:T(8,128)S(1)} copy-done((f32[512,3072]{1,0:T(8,128)S(1)}, f32[512,3072]{1,0:T(8,128)}, u32[]{:S(2)}) %copy-start) | copy-done | bytes 6291480
  4.6 2.1 %first_solve.1.own_ref = bf16[512,512]{1,0:T(8,128)(2,1)} custom-call(f32[512,3072]{1,0:T(8,128)S(1)} %copy-done, bf16[2,512,512]{2,1,0:T(8,128)(2,1)S(1)} %copy-done.4), custom_call_target="tpu_custom_call" | custom-call | flops 805306368 | bytes 4194304 | tf_op jit(solution)/shard_map/first_solve/pallas_call | solution.py:41
  6.7 2.5 %collective-permute-start = (bf16[512,512]{1,0:T(8,128)(2,1)}, bf16[512,512]{1,0:T(8,128)(2,1)}, u32[]{:S(2)}, u32[]{:S(2)}) collective-permute-start(bf16[512,512]{1,0:T(8,128)(2,1)} %first_solve.1.own_ref), channel_id=1, source_target_pairs={{0,1},{2,3},{4,5},{6,7},{8,9},{10,11},{12,13},{14,15},{16,17},{18,... | collective-permute-start | bytes 1572872 | tf_op jit(solution)/shard_map/ppermute | solution.py:193
  12.5 2.8 %copy-done.1 = f32[512,3072]{1,0:T(8,128)S(1)} copy-done((f32[512,3072]{1,0:T(8,128)S(1)}, f32[512,3072]{1,0:T(8,128)}, u32[]{:S(2)}) %copy-start.1) | copy-done | bytes 6291480
  16.5 5.4 %second_solve.1 = (bf16[128,512]{1,0:T(8,128)(2,1)S(1)}, bf16[128,512]{1,0:T(8,128)(2,1)}, bf16[128,512]{1,0:T(8,128)(2,1)S(1)}, bf16[128,512]{1,0:T(8,128)(2,1)S(1)}) custom-call(s32[7]{0:T(128)S(1)} %stack.52.flags, f32[512,3072]{1,0:T(8,128)S(1)} %copy-done.1, bf16[2,512,512]{2,1,0:T(8,128)(2,1)S(1)} %copy-done.5, bf16[512,512]{1,0:T(8,128)(2,1)} %first_solve.1.own_ref, ...), custom_call_target="tpu_custom_call" | custom-call | flops 1073741824 | bytes 4194304 | tf_op jit(solution)/shard_map/second_solve/pallas_call | solution.py:69
  21.9 4.5 %collective-permute-start.2 = (bf16[128,512]{1,0:T(8,128)(2,1)}, bf16[128,512]{1,0:T(8,128)(2,1)}, u32[]{:S(2)}, u32[]{:S(2)}) collective-permute-start(bf16[128,512]{1,0:T(8,128)(2,1)} %get-tuple-element.10), channel_id=1, source_target_pairs={{0,16},{1,17},{2,18},{3,19},{4,20},{5,21},{6,22},{7,23},{8,24},{9,... | collective-permute-start | bytes 393224 | tf_op jit(solution)/shard_map/ppermute | solution.py:196
  26.3 3.3 %collective-permute-start.3 = (bf16[128,512]{1,0:T(8,128)(2,1)S(1)}, bf16[128,512]{1,0:T(8,128)(2,1)}, u32[]{:S(2)}, u32[]{:S(2)}) collective-permute-start(bf16[128,512]{1,0:T(8,128)(2,1)S(1)} %get-tuple-element.11), channel_id=1, source_target_pairs={{0,32},{1,33},{2,34},{3,35},{4,36},{5,37},{6,38},{7,39},{8,40},{9,... | collective-permute-start | bytes 393224 | tf_op jit(solution)/shard_map/ppermute | solution.py:196
  34.4 4.9 %collective-permute-start.7 = (bf16[32,512]{1,0:T(8,128)(2,1)S(1)}, bf16[32,512]{1,0:T(8,128)(2,1)S(1)}, u32[]{:S(2)}, u32[]{:S(2)}) collective-permute-start(bf16[32,512]{1,0:T(8,128)(2,1)S(1)} %get-tuple-element.22), channel_id=1, source_target_pairs={{0,12},{1,13},{2,14},{3,15},{16,28},{17,29},{18,30},{19,31},{32,44... | collective-permute-start | bytes 98312 | tf_op jit(solution)/shard_map/ppermute | solution.py:200
  44.4 3.1 %collective-permute-done.8 = bf16[32,512]{1,0:T(8,128)(2,1)S(1)} collective-permute-done((bf16[32,512]{1,0:T(8,128)(2,1)S(1)}, bf16[32,512]{1,0:T(8,128)(2,1)S(1)}, u32[]{:S(2)}, u32[]{:S(2)}) %collective-permute-start.8) | collective-permute-done | bytes 32800 | tf_op jit(solution)/shard_map/ppermute | solution.py:202
  48.8 6.1 %collective-permute-done.9 = bf16[2,32,512]{2,1,0:T(8,128)(2,1)S(1)} collective-permute-done((bf16[2,32,512]{2,1,0:T(8,128)(2,1)S(1)}, bf16[2,32,512]{2,1,0:T(8,128)(2,1)S(1)}, u32[]{:S(2)}, u32[]{:S(2)}) %collective-permute-start.9) | collective-permute-done | bytes 65568 | tf_op jit(solution)/shard_map/ppermute | solution.py:204
  54.9 2.6 %collective-permute-start.12 = (bf16[2,32,512]{2,1,0:T(8,128)(2,1)S(1)}, bf16[2,32,512]{2,1,0:T(8,128)(2,1)S(1)}, u32[]{:S(2)}, u32[]{:S(2)}) collective-permute-start(bf16[2,32,512]{2,1,0:T(8,128)(2,1)S(1)} %broadcast_select_fusion.own), channel_id=1, source_target_pairs={{0,8},{4,12},{8,0},{12,4},{1,9},{5,13},{9,1},{13,5},{2,10},{6,14},... | collective-permute-start | bytes 196616 | tf_op jit(solution)/shard_map/ppermute | solution.py:185
  57.5 2.5 %collective-permute-start.11 = (bf16[2,32,512]{2,1,0:T(8,128)(2,1)S(1)}, bf16[2,32,512]{2,1,0:T(8,128)(2,1)S(1)}, u32[]{:S(2)}, u32[]{:S(2)}) collective-permute-start(bf16[2,32,512]{2,1,0:T(8,128)(2,1)S(1)} %broadcast_select_fusion.own), channel_id=1, source_target_pairs={{0,12},{4,0},{8,4},{12,8},{1,13},{5,1},{9,5},{13,9},{2,14},{6,2},{... | collective-permute-start | bytes 196616 | tf_op jit(solution)/shard_map/ppermute | solution.py:185
  61.9 3.6 %collective-permute-done.10.up = bf16[2,32,512]{2,1,0:T(8,128)(2,1)S(1)} collective-permute-done((bf16[2,32,512]{2,1,0:T(8,128)(2,1)S(1)}, bf16[2,32,512]{2,1,0:T(8,128)(2,1)S(1)}, u32[]{:S(2)}, u32[]{:S(2)}) %collective-permute-start.10) | collective-permute-done | bytes 65568 | tf_op jit(solution)/shard_map/ppermute | solution.py:185
  66.0 3.8 %collective-permute-start.14 = (bf16[4,2,32,512]{3,2,1,0:T(8,128)(2,1)S(1)}, bf16[4,2,32,512]{3,2,1,0:T(8,128)(2,1)S(1)}, u32[]{:S(2)}, u32[]{:S(2)}) collective-permute-start(bf16[4,2,32,512]{3,2,1,0:T(8,128)(2,1)S(1)} %shard_map.50.own), channel_id=1, source_target_pairs={{0,48},{16,0},{32,16},{48,32},{1,49},{17,1},{33,17},{49,33},{2,50}... | collective-permute-start | bytes 786440 | tf_op jit(solution)/shard_map/ppermute | solution.py:185
  69.8 3.9 %collective-permute-done.14.down = bf16[4,2,32,512]{3,2,1,0:T(8,128)(2,1)S(1)} collective-permute-done((bf16[4,2,32,512]{3,2,1,0:T(8,128)(2,1)S(1)}, bf16[4,2,32,512]{3,2,1,0:T(8,128)(2,1)S(1)}, u32[]{:S(2)}, u32[]{:S(2)}) %collective-permute-start.14) | collective-permute-done | bytes 262176 | tf_op jit(solution)/shard_map/ppermute | solution.py:185
  73.7 3.8 %collective-permute-start.16 = (bf16[2,2,32,512]{3,2,1,0:T(8,128)(2,1)S(1)}, bf16[2,2,32,512]{3,2,1,0:T(8,128)(2,1)S(1)}, u32[]{:S(2)}, u32[]{:S(2)}) collective-permute-start(bf16[2,2,32,512]{3,2,1,0:T(8,128)(2,1)S(1)} %slice.53), channel_id=1, source_target_pairs={{0,48},{16,0},{32,16},{48,32},{1,49},{17,1},{33,17},{49,33},{2,50}... | collective-permute-start | bytes 393224 | tf_op jit(solution)/shard_map/ppermute | solution.py:185
  77.6 2.4 %collective-permute-done.16.far_b = bf16[2,2,32,512]{3,2,1,0:T(8,128)(2,1)S(1)} collective-permute-done((bf16[2,2,32,512]{3,2,1,0:T(8,128)(2,1)S(1)}, bf16[2,2,32,512]{3,2,1,0:T(8,128)(2,1)S(1)}, u32[]{:S(2)}, u32[]{:S(2)}) %collective-permute-start.16) | collective-permute-done | bytes 131104 | tf_op jit(solution)/shard_map/ppermute | solution.py:185
  80.0 3.7 %collective-permute-done.15.far_a = bf16[2,2,32,512]{3,2,1,0:T(8,128)(2,1)S(1)} collective-permute-done((bf16[2,2,32,512]{3,2,1,0:T(8,128)(2,1)S(1)}, bf16[2,2,32,512]{3,2,1,0:T(8,128)(2,1)S(1)}, u32[]{:S(2)}, u32[]{:S(2)}) %collective-permute-start.15) | collective-permute-done | bytes 131104 | tf_op jit(solution)/shard_map/ppermute | solution.py:185
  86.4 2.1 %collective-permute-start.22 = (bf16[512,512]{1,0:T(8,128)(2,1)}, bf16[512,512]{1,0:T(8,128)(2,1)S(1)}, u32[]{:S(2)}, u32[]{:S(2)}) collective-permute-start(bf16[512,512]{1,0:T(8,128)(2,1)} %get-tuple-element.16), channel_id=1, source_target_pairs={{0,64},{64,0},{1,65},{65,1},{2,66},{66,2},{3,67},{67,3},{4,68},{68... | collective-permute-start | bytes 1572872 | tf_op jit(solution)/shard_map/ppermute | solution.py:191
  90.5 10.9 %collective-permute-done.23.other = bf16[512,512]{1,0:T(8,128)(2,1)S(1)} collective-permute-done((bf16[512,512]{1,0:T(8,128)(2,1)}, bf16[512,512]{1,0:T(8,128)(2,1)S(1)}, u32[]{:S(2)}, u32[]{:S(2)}) %collective-permute-start.23) | collective-permute-done | bytes 524320 | tf_op jit(solution)/shard_map/ppermute | solution.py:189
  101.4 2.0 %collective-permute-start.18 = (bf16[512,512]{1,0:T(8,128)(2,1)}, bf16[512,512]{1,0:T(8,128)(2,1)S(1)}, u32[]{:S(2)}, u32[]{:S(2)}) collective-permute-start(bf16[512,512]{1,0:T(8,128)(2,1)} %get-tuple-element.20), channel_id=1, source_target_pairs={{0,64},{64,0},{1,65},{65,1},{2,66},{66,2},{3,67},{67,3},{4,68},{68... | collective-permute-start | bytes 1572872 | tf_op jit(solution)/shard_map/ppermute | solution.py:191
  105.2 2.8 %copy-done.2 = f32[512,3072]{1,0:T(8,128)S(1)} copy-done((f32[512,3072]{1,0:T(8,128)S(1)}, f32[512,3072]{1,0:T(8,128)}, u32[]{:S(2)}) %copy-start.2) | copy-done | bytes 6291480
  107.9 3.3 %update.6.rest_0_ = f32[512,3072]{1,0:T(8,128)} custom-call(s32[7]{0:T(128)S(1)} %stack.52.flags, bf16[512,512]{1,0:T(8,128)(2,1)S(1)} %get-tuple-element.14.left, bf16[512,512]{1,0:T(8,128)(2,1)S(1)} %get-tuple-element.15.right, f32[512,3072]{1,0:T(8,128)S(1)} %copy-done.2, bf16[3072,512]{1,0:T(8,128)(2,1)S(1)} %copy-done.3, ...), custom_call_target="tpu_custom_call" | custom-call | flops 536870912 | bytes 4194304 | tf_op jit(solution)/shard_map/update/pallas_call | solution.py:154
  112.6 2.4 %update.7.rest_0_ = f32[512,3072]{1,0:T(8,128)} custom-call(s32[7]{0:T(128)S(1)} %stack.52.flags, bf16[512,512]{1,0:T(8,128)(2,1)S(1)} %get-tuple-element.14.left, bf16[512,512]{1,0:T(8,128)(2,1)S(1)} %get-tuple-element.15.right, f32[512,3072]{1,0:T(8,128)S(1)} %copy-done.2, bf16[3072,512]{1,0:T(8,128)(2,1)S(1)} %copy-done.3, ...), custom_call_target="tpu_custom_call", output_to_operand_aliasing={{}: (6, {})} | custom-call | flops 536870912 | bytes 4194304 | tf_op jit(solution)/shard_map/update/pallas_call | solution.py:154
  115.0 8.8 %collective-permute-done.21.other = bf16[512,512]{1,0:T(8,128)(2,1)S(1)} collective-permute-done((bf16[512,512]{1,0:T(8,128)(2,1)}, bf16[512,512]{1,0:T(8,128)(2,1)S(1)}, u32[]{:S(2)}, u32[]{:S(2)}) %collective-permute-start.21) | collective-permute-done | bytes 524320 | tf_op jit(solution)/shard_map/ppermute | solution.py:191
  123.8 2.4 %update.8.rest_0_ = f32[512,3072]{1,0:T(8,128)} custom-call(s32[7]{0:T(128)S(1)} %stack.52.flags, bf16[512,512]{1,0:T(8,128)(2,1)S(1)} %get-tuple-element.14.left, bf16[512,512]{1,0:T(8,128)(2,1)S(1)} %get-tuple-element.15.right, f32[512,3072]{1,0:T(8,128)S(1)} %copy-done.2, bf16[3072,512]{1,0:T(8,128)(2,1)S(1)} %copy-done.3, ...), custom_call_target="tpu_custom_call", output_to_operand_aliasing={{}: (6, {})} | custom-call | flops 536870912 | bytes 4194304 | tf_op jit(solution)/shard_map/update/pallas_call | solution.py:154
  126.3 8.8 %collective-permute-done.20.other = bf16[512,512]{1,0:T(8,128)(2,1)S(1)} collective-permute-done((bf16[512,512]{1,0:T(8,128)(2,1)}, bf16[512,512]{1,0:T(8,128)(2,1)S(1)}, u32[]{:S(2)}, u32[]{:S(2)}) %collective-permute-start.20) | collective-permute-done | bytes 524320 | tf_op jit(solution)/shard_map/ppermute | solution.py:191
  135.1 2.4 %update.9.rest_0_ = f32[512,3072]{1,0:T(8,128)} custom-call(s32[7]{0:T(128)S(1)} %stack.52.flags, bf16[512,512]{1,0:T(8,128)(2,1)S(1)} %get-tuple-element.14.left, bf16[512,512]{1,0:T(8,128)(2,1)S(1)} %get-tuple-element.15.right, f32[512,3072]{1,0:T(8,128)S(1)} %copy-done.2, bf16[3072,512]{1,0:T(8,128)(2,1)S(1)} %copy-done.3, ...), custom_call_target="tpu_custom_call", output_to_operand_aliasing={{}: (6, {})} | custom-call | flops 536870912 | bytes 4194304 | tf_op jit(solution)/shard_map/update/pallas_call | solution.py:154
  137.5 8.8 %collective-permute-done.19.other = bf16[512,512]{1,0:T(8,128)(2,1)S(1)} collective-permute-done((bf16[512,512]{1,0:T(8,128)(2,1)}, bf16[512,512]{1,0:T(8,128)(2,1)S(1)}, u32[]{:S(2)}, u32[]{:S(2)}) %collective-permute-start.19) | collective-permute-done | bytes 524320 | tf_op jit(solution)/shard_map/ppermute | solution.py:191
  146.3 2.4 %update.10.rest_0_ = f32[512,3072]{1,0:T(8,128)} custom-call(s32[7]{0:T(128)S(1)} %stack.52.flags, bf16[512,512]{1,0:T(8,128)(2,1)S(1)} %get-tuple-element.14.left, bf16[512,512]{1,0:T(8,128)(2,1)S(1)} %get-tuple-element.15.right, f32[512,3072]{1,0:T(8,128)S(1)} %copy-done.2, bf16[3072,512]{1,0:T(8,128)(2,1)S(1)} %copy-done.3, ...), custom_call_target="tpu_custom_call", output_to_operand_aliasing={{}: (6, {})} | custom-call | flops 536870912 | bytes 4194304 | tf_op jit(solution)/shard_map/update/pallas_call | solution.py:154
  148.7 8.3 %collective-permute-done.18.other = bf16[512,512]{1,0:T(8,128)(2,1)S(1)} collective-permute-done((bf16[512,512]{1,0:T(8,128)(2,1)}, bf16[512,512]{1,0:T(8,128)(2,1)S(1)}, u32[]{:S(2)}, u32[]{:S(2)}) %collective-permute-start.18) | collective-permute-done | bytes 524320 | tf_op jit(solution)/shard_map/ppermute | solution.py:191
  157.1 2.4 %update.11 = f32[512,3072]{1,0:T(8,128)} custom-call(s32[7]{0:T(128)S(1)} %stack.52.flags, bf16[512,512]{1,0:T(8,128)(2,1)S(1)} %get-tuple-element.14.left, bf16[512,512]{1,0:T(8,128)(2,1)S(1)} %get-tuple-element.15.right, f32[512,3072]{1,0:T(8,128)S(1)} %copy-done.2, bf16[3072,512]{1,0:T(8,128)(2,1)S(1)} %copy-done.3, ...), custom_call_target="tpu_custom_call", output_to_operand_aliasing={{}: (6, {})} | custom-call | flops 536870912 | bytes 4194304 | tf_op jit(solution)/shard_map/update/pallas_call | solution.py:154
  (49 shorter events, 27.1 us)
Async XLA Ops:
  0.6 2.8 %copy-start = (f32[512,3072]{1,0:T(8,128)S(1)}, f32[512,3072]{1,0:T(8,128)}, u32[]{:S(2)}) copy-start(f32[512,3072]{1,0:T(8,128)} %rhs.11) | copy-start | bytes 18874372
  3.4 1.2 copy-start.4
  4.6 4.6 %copy-start.3 = (bf16[3072,512]{1,0:T(8,128)(2,1)S(1)}, bf16[3072,512]{1,0:T(8,128)(2,1)}, u32[]{:S(2)}) copy-start(bf16[3072,512]{1,0:T(8,128)(2,1)} %own.11) | copy-start | bytes 9437188
  6.7 5.8 %collective-permute-start = (bf16[512,512]{1,0:T(8,128)(2,1)}, bf16[512,512]{1,0:T(8,128)(2,1)}, u32[]{:S(2)}, u32[]{:S(2)}) collective-permute-start(bf16[512,512]{1,0:T(8,128)(2,1)} %first_solve.1.own_ref), channel_id=1, source_target_pairs={{0,1},{2,3},{4,5},{6,7},{8,9},{10,11},{12,13},{14,15},{16,17},{18,... | collective-permute-start | bytes 1572872 | tf_op jit(solution)/shard_map/ppermute | solution.py:193
  10.9 1.5 collective-permute-start.1
  12.5 2.8 %copy-start.1 = (f32[512,3072]{1,0:T(8,128)S(1)}, f32[512,3072]{1,0:T(8,128)}, u32[]{:S(2)}) copy-start(f32[512,3072]{1,0:T(8,128)} %rhs.11) | copy-start | bytes 18874372
  15.3 1.2 copy-start.5
  21.9 9.7 %collective-permute-start.2 = (bf16[128,512]{1,0:T(8,128)(2,1)}, bf16[128,512]{1,0:T(8,128)(2,1)}, u32[]{:S(2)}, u32[]{:S(2)}) collective-permute-start(bf16[128,512]{1,0:T(8,128)(2,1)} %get-tuple-element.10), channel_id=1, source_target_pairs={{0,16},{1,17},{2,18},{3,19},{4,20},{5,21},{6,22},{7,23},{8,24},{9,... | collective-permute-start | bytes 393224 | tf_op jit(solution)/shard_map/ppermute | solution.py:196
  26.3 5.2 %collective-permute-start.3 = (bf16[128,512]{1,0:T(8,128)(2,1)S(1)}, bf16[128,512]{1,0:T(8,128)(2,1)}, u32[]{:S(2)}, u32[]{:S(2)}) collective-permute-start(bf16[128,512]{1,0:T(8,128)(2,1)S(1)} %get-tuple-element.11), channel_id=1, source_target_pairs={{0,32},{1,33},{2,34},{3,35},{4,36},{5,37},{6,38},{7,39},{8,40},{9,... | collective-permute-start | bytes 393224 | tf_op jit(solution)/shard_map/ppermute | solution.py:196
  29.6 3.8 %collective-permute-start.4 = (bf16[128,512]{1,0:T(8,128)(2,1)S(1)}, bf16[128,512]{1,0:T(8,128)(2,1)}, u32[]{:S(2)}, u32[]{:S(2)}) collective-permute-start(bf16[128,512]{1,0:T(8,128)(2,1)S(1)} %get-tuple-element.12), channel_id=1, source_target_pairs={{0,48},{1,49},{2,50},{3,51},{4,52},{5,53},{6,54},{7,55},{8,56},{9,... | collective-permute-start | bytes 393224 | tf_op jit(solution)/shard_map/ppermute | solution.py:196
  34.4 7.5 %collective-permute-start.7 = (bf16[32,512]{1,0:T(8,128)(2,1)S(1)}, bf16[32,512]{1,0:T(8,128)(2,1)S(1)}, u32[]{:S(2)}, u32[]{:S(2)}) collective-permute-start(bf16[32,512]{1,0:T(8,128)(2,1)S(1)} %get-tuple-element.22), channel_id=1, source_target_pairs={{0,12},{1,13},{2,14},{3,15},{16,28},{17,29},{18,30},{19,31},{32,44... | collective-permute-start | bytes 98312 | tf_op jit(solution)/shard_map/ppermute | solution.py:200
  39.3 2.9 %collective-permute-start.6 = (bf16[32,512]{1,0:T(8,128)(2,1)S(1)}, bf16[32,512]{1,0:T(8,128)(2,1)S(1)}, u32[]{:S(2)}, u32[]{:S(2)}) collective-permute-start(bf16[32,512]{1,0:T(8,128)(2,1)S(1)} %get-tuple-element.23), channel_id=1, source_target_pairs={{0,8},{1,9},{2,10},{3,11},{16,24},{17,25},{18,26},{19,27},{32,40},... | collective-permute-start | bytes 98312 | tf_op jit(solution)/shard_map/ppermute | solution.py:200
  40.6 2.9 %collective-permute-start.5 = (bf16[32,512]{1,0:T(8,128)(2,1)S(1)}, bf16[32,512]{1,0:T(8,128)(2,1)S(1)}, u32[]{:S(2)}, u32[]{:S(2)}) collective-permute-start(bf16[32,512]{1,0:T(8,128)(2,1)S(1)} %get-tuple-element.24), channel_id=1, source_target_pairs={{0,4},{1,5},{2,6},{3,7},{16,20},{17,21},{18,22},{19,23},{32,36},{3... | collective-permute-start | bytes 98312 | tf_op jit(solution)/shard_map/ppermute | solution.py:200
  43.5 4.0 %collective-permute-start.8 = (bf16[32,512]{1,0:T(8,128)(2,1)S(1)}, bf16[32,512]{1,0:T(8,128)(2,1)S(1)}, u32[]{:S(2)}, u32[]{:S(2)}) collective-permute-start(bf16[32,512]{1,0:T(8,128)(2,1)S(1)} %slice_select_fusion), channel_id=1, source_target_pairs={{0,64},{64,0},{1,65},{65,1},{2,66},{66,2},{3,67},{67,3},{4,68},{68... | collective-permute-start | bytes 98312 | tf_op jit(solution)/shard_map/ppermute | solution.py:202
  47.5 7.4 %collective-permute-start.9 = (bf16[2,32,512]{2,1,0:T(8,128)(2,1)S(1)}, bf16[2,32,512]{2,1,0:T(8,128)(2,1)S(1)}, u32[]{:S(2)}, u32[]{:S(2)}) collective-permute-start(bf16[2,32,512]{2,1,0:T(8,128)(2,1)S(1)} %pad_maximum_fusion), channel_id=1, source_target_pairs={{64,2},{0,66},{65,3},{1,67},{68,6},{4,70},{69,7},{5,71},{72,10},{8... | collective-permute-start | bytes 196616 | tf_op jit(solution)/shard_map/ppermute | solution.py:204
  54.9 5.8 %collective-permute-start.12 = (bf16[2,32,512]{2,1,0:T(8,128)(2,1)S(1)}, bf16[2,32,512]{2,1,0:T(8,128)(2,1)S(1)}, u32[]{:S(2)}, u32[]{:S(2)}) collective-permute-start(bf16[2,32,512]{2,1,0:T(8,128)(2,1)S(1)} %broadcast_select_fusion.own), channel_id=1, source_target_pairs={{0,8},{4,12},{8,0},{12,4},{1,9},{5,13},{9,1},{13,5},{2,10},{6,14},... | collective-permute-start | bytes 196616 | tf_op jit(solution)/shard_map/ppermute | solution.py:185
  57.5 4.4 %collective-permute-start.11 = (bf16[2,32,512]{2,1,0:T(8,128)(2,1)S(1)}, bf16[2,32,512]{2,1,0:T(8,128)(2,1)S(1)}, u32[]{:S(2)}, u32[]{:S(2)}) collective-permute-start(bf16[2,32,512]{2,1,0:T(8,128)(2,1)S(1)} %broadcast_select_fusion.own), channel_id=1, source_target_pairs={{0,12},{4,0},{8,4},{12,8},{1,13},{5,1},{9,5},{13,9},{2,14},{6,2},{... | collective-permute-start | bytes 196616 | tf_op jit(solution)/shard_map/ppermute | solution.py:185
  60.0 5.5 %collective-permute-start.10 = (bf16[2,32,512]{2,1,0:T(8,128)(2,1)S(1)}, bf16[2,32,512]{2,1,0:T(8,128)(2,1)S(1)}, u32[]{:S(2)}, u32[]{:S(2)}) collective-permute-start(bf16[2,32,512]{2,1,0:T(8,128)(2,1)S(1)} %broadcast_select_fusion.own), channel_id=1, source_target_pairs={{0,4},{4,8},{8,12},{12,0},{1,5},{5,9},{9,13},{13,1},{2,6},{6,10},{... | collective-permute-start | bytes 196616 | tf_op jit(solution)/shard_map/ppermute | solution.py:185
  66.0 7.7 %collective-permute-start.14 = (bf16[4,2,32,512]{3,2,1,0:T(8,128)(2,1)S(1)}, bf16[4,2,32,512]{3,2,1,0:T(8,128)(2,1)S(1)}, u32[]{:S(2)}, u32[]{:S(2)}) collective-permute-start(bf16[4,2,32,512]{3,2,1,0:T(8,128)(2,1)S(1)} %shard_map.50.own), channel_id=1, source_target_pairs={{0,48},{16,0},{32,16},{48,32},{1,49},{17,1},{33,17},{49,33},{2,50}... | collective-permute-start | bytes 786440 | tf_op jit(solution)/shard_map/ppermute | solution.py:185
  69.8 7.7 %collective-permute-start.13 = (bf16[4,2,32,512]{3,2,1,0:T(8,128)(2,1)S(1)}, bf16[4,2,32,512]{3,2,1,0:T(8,128)(2,1)S(1)}, u32[]{:S(2)}, u32[]{:S(2)}) collective-permute-start(bf16[4,2,32,512]{3,2,1,0:T(8,128)(2,1)S(1)} %shard_map.50.own), channel_id=1, source_target_pairs={{0,16},{16,32},{32,48},{48,0},{1,17},{17,33},{33,49},{49,1},{2,18}... | collective-permute-start | bytes 786440 | tf_op jit(solution)/shard_map/ppermute | solution.py:185
  73.7 6.3 %collective-permute-start.16 = (bf16[2,2,32,512]{3,2,1,0:T(8,128)(2,1)S(1)}, bf16[2,2,32,512]{3,2,1,0:T(8,128)(2,1)S(1)}, u32[]{:S(2)}, u32[]{:S(2)}) collective-permute-start(bf16[2,2,32,512]{3,2,1,0:T(8,128)(2,1)S(1)} %slice.53), channel_id=1, source_target_pairs={{0,48},{16,0},{32,16},{48,32},{1,49},{17,1},{33,17},{49,33},{2,50}... | collective-permute-start | bytes 393224 | tf_op jit(solution)/shard_map/ppermute | solution.py:185
  77.5 6.2 %collective-permute-start.15 = (bf16[2,2,32,512]{3,2,1,0:T(8,128)(2,1)S(1)}, bf16[2,2,32,512]{3,2,1,0:T(8,128)(2,1)S(1)}, u32[]{:S(2)}, u32[]{:S(2)}) collective-permute-start(bf16[2,2,32,512]{3,2,1,0:T(8,128)(2,1)S(1)} %slice.52), channel_id=1, source_target_pairs={{0,16},{16,32},{32,48},{48,0},{1,17},{17,33},{33,49},{49,1},{2,18}... | collective-permute-start | bytes 393224 | tf_op jit(solution)/shard_map/ppermute | solution.py:185
  84.4 17.0 %collective-permute-start.17 = (bf16[2,512,512]{2,1,0:T(8,128)(2,1)S(1)}, bf16[2,512,512]{2,1,0:T(8,128)(2,1)S(1)}, u32[]{:S(2)}, u32[]{:S(2)}) collective-permute-start(bf16[2,512,512]{2,1,0:T(8,128)(2,1)S(1)} %bitcast.12), channel_id=1, source_target_pairs={{0,1},{1,0},{2,3},{3,2},{4,5},{5,4},{6,7},{7,6},{8,9},{9,8},{10,11... | collective-permute-start | bytes 3145736 | tf_op jit(solution)/shard_map/ppermute | solution.py:212
  84.5 16.9 %collective-permute-start.23 = (bf16[512,512]{1,0:T(8,128)(2,1)}, bf16[512,512]{1,0:T(8,128)(2,1)S(1)}, u32[]{:S(2)}, u32[]{:S(2)}) collective-permute-start(bf16[512,512]{1,0:T(8,128)(2,1)} %get-tuple-element.21), channel_id=1, source_target_pairs={{2,66},{3,67},{4,68},{5,69},{6,70},{7,71},{8,72},{9,73},{10,74},{1... | collective-permute-start | bytes 1572872 | tf_op jit(solution)/shard_map/ppermute | solution.py:189
  86.4 26.2 %collective-permute-start.22 = (bf16[512,512]{1,0:T(8,128)(2,1)}, bf16[512,512]{1,0:T(8,128)(2,1)S(1)}, u32[]{:S(2)}, u32[]{:S(2)}) collective-permute-start(bf16[512,512]{1,0:T(8,128)(2,1)} %get-tuple-element.16), channel_id=1, source_target_pairs={{0,64},{64,0},{1,65},{65,1},{2,66},{66,2},{3,67},{67,3},{4,68},{68... | collective-permute-start | bytes 1572872 | tf_op jit(solution)/shard_map/ppermute | solution.py:191
  88.5 35.3 %collective-permute-start.21 = (bf16[512,512]{1,0:T(8,128)(2,1)}, bf16[512,512]{1,0:T(8,128)(2,1)S(1)}, u32[]{:S(2)}, u32[]{:S(2)}) collective-permute-start(bf16[512,512]{1,0:T(8,128)(2,1)} %get-tuple-element.17), channel_id=1, source_target_pairs={{0,64},{64,0},{1,65},{65,1},{2,66},{66,2},{3,67},{67,3},{4,68},{68... | collective-permute-start | bytes 1572872 | tf_op jit(solution)/shard_map/ppermute | solution.py:191
  88.6 46.5 %collective-permute-start.20 = (bf16[512,512]{1,0:T(8,128)(2,1)}, bf16[512,512]{1,0:T(8,128)(2,1)S(1)}, u32[]{:S(2)}, u32[]{:S(2)}) collective-permute-start(bf16[512,512]{1,0:T(8,128)(2,1)} %get-tuple-element.18), channel_id=1, source_target_pairs={{0,64},{64,0},{1,65},{65,1},{2,66},{66,2},{3,67},{67,3},{4,68},{68... | collective-permute-start | bytes 1572872 | tf_op jit(solution)/shard_map/ppermute | solution.py:191
  101.4 44.9 %collective-permute-start.19 = (bf16[512,512]{1,0:T(8,128)(2,1)}, bf16[512,512]{1,0:T(8,128)(2,1)S(1)}, u32[]{:S(2)}, u32[]{:S(2)}) collective-permute-start(bf16[512,512]{1,0:T(8,128)(2,1)} %get-tuple-element.19), channel_id=1, source_target_pairs={{0,64},{64,0},{1,65},{65,1},{2,66},{66,2},{3,67},{67,3},{4,68},{68... | collective-permute-start | bytes 1572872 | tf_op jit(solution)/shard_map/ppermute | solution.py:191
  101.4 55.7 %collective-permute-start.18 = (bf16[512,512]{1,0:T(8,128)(2,1)}, bf16[512,512]{1,0:T(8,128)(2,1)S(1)}, u32[]{:S(2)}, u32[]{:S(2)}) collective-permute-start(bf16[512,512]{1,0:T(8,128)(2,1)} %get-tuple-element.20), channel_id=1, source_target_pairs={{0,64},{64,0},{1,65},{65,1},{2,66},{66,2},{3,67},{67,3},{4,68},{68... | collective-permute-start | bytes 1572872 | tf_op jit(solution)/shard_map/ppermute | solution.py:191
  105.1 2.8 %copy-start.2 = (f32[512,3072]{1,0:T(8,128)S(1)}, f32[512,3072]{1,0:T(8,128)}, u32[]{:S(2)}) copy-start(f32[512,3072]{1,0:T(8,128)} %rhs.11) | copy-start | bytes 18874372

commit v2 on v0

v2 whole, which is shorter than its diff:
```python
import functools

import jax
import jax.numpy as jnp
from jax import lax
from jax.experimental import pallas as pl
from jax.experimental.pallas import tpu as pltpu
from jax.sharding import Mesh
from jax.sharding import PartitionSpec as P


NB = 512
COL = ("z", "y", "xh", "core")
ALL = ("row",) + COL
NT = (((1,), (1,)), ((), ()))
F32 = jnp.float32
BF16 = jnp.bfloat16
CUTS = (0, 512, 1280, 2048, 2560, 2816, 3072)
SIZES = tuple(b - a for a, b in zip(CUTS[:-1], CUTS[1:]))
GROUPS = ((0, 1, 2), (3,), (4,), (5,))
TILE = 256
VMEM_BYTES = 67043328

VMEM = pl.BlockSpec(memory_space=pltpu.VMEM)
HBM = pl.BlockSpec(memory_space=pltpu.HBM)


def column():
    index = lax.axis_index(COL[0])
    for name, size in zip(COL[1:], (4, 2, 2)):
        index = index * size + lax.axis_index(name)
    return index


def dot_nt(a, b):
    return lax.dot_general(a, b, NT, preferred_element_type=F32)


def times_inverse(x, inverse):
    high = x.astype(BF16)
    rest = x - high.astype(F32)
    mid = rest.astype(BF16)
    low = (rest - mid.astype(F32)).astype(BF16)
    parts = dot_nt(jnp.concatenate([low, mid, high], axis=0), inverse)
    count = x.shape[0]
    return parts[:count] + parts[count : 2 * count] + parts[2 * count :]


def call(body, operands, in_specs, outs, scratch=(), flops=1 << 20, room=None):
    limit = 12 << 20 if room is None else VMEM_BYTES - (room << 10)
    return pl.pallas_call(
        body,
        in_specs=in_specs,
        out_specs=[VMEM] * len(outs),
        out_shape=outs,
        scratch_shapes=list(scratch),
        compiler_params=pltpu.CompilerParams(vmem_limit_bytes=limit),
        cost_estimate=pl.CostEstimate(flops=flops, bytes_accessed=1 << 20, transcendentals=0),
    )(*operands)


def shape(*dims, dtype=BF16):
    return jax.ShapeDtypeStruct(dims, dtype)


def cut_body(panel, out, sem):
    copy = pltpu.make_async_copy(panel.at[pl.ds(CUTS[0], SIZES[0])], out, sem)
    copy.start()
    copy.wait()


def first_body(rhs, inv, panel, base, low, piece, rhs_in, inv_in, sems):
    cut = pltpu.make_async_copy(panel.at[pl.ds(CUTS[1], SIZES[1])], piece, sems.at[0])

    @pl.when(column() < 2)
    def _():
        loads = [
            pltpu.make_async_copy(inv.at[lax.axis_index("core")], inv_in, sems.at[1]),
            pltpu.make_async_copy(rhs.at[:, pl.ds(0, NB)], rhs_in, sems.at[2]),
        ]
        for load in loads:
            load.start()
        for load in loads:
            load.wait()
        value = times_inverse(rhs_in[...], inv_in[...])
        base[...] = value
        low[...] = value.astype(BF16)

    cut.start()
    cut.wait()


def second_body(base, low, arrived, block, sent, inv, panel, *refs):
    quarters, cuts, inv_in, sems = refs[:4], refs[4:-2], refs[-2], refs[-1]
    copies = [
        pltpu.make_async_copy(panel.at[pl.ds(CUTS[k], SIZES[k])], out, sems.at[k])
        for k, out in enumerate(cuts, 2)
    ]
    part = NB // 4

    @pl.when(column() == 0)
    def _():
        for q in range(4):
            quarters[q][...] = low[pl.ds(q * part, part), :]

    @pl.when(column() == 1)
    def _():
        load = pltpu.make_async_copy(inv.at[1], inv_in, sems.at[0])
        load.start()
        below = jnp.where(lax.axis_index("row") == 0, block[...], sent[...])
        load.wait()
        product = dot_nt(arrived[...], below)
        value = (base[...] - times_inverse(product, inv_in[...])).astype(BF16)
        for q in range(4):
            quarters[q][...] = value[q * part : (q + 1) * part]

    for copy in copies:
        copy.start()
    for copy in copies:
        copy.wait()


def choose_body(place, *refs):
    given, outs = refs[:4], refs[4:]
    part = given[0].shape[0] // len(outs)
    for q in range(4):

        @pl.when(lax.axis_index(place) == q)
        def _():
            for i, out in enumerate(outs):
                out[...] = given[q][pl.ds(i * part, part), :]


def select_body(near, far, out):
    @pl.when(lax.axis_index("xh") == 0)
    def _():
        out[...] = near[...]

    @pl.when(lax.axis_index("xh") == 1)
    def _():
        out[...] = far[...]


def ring_body(own, up, down, far, out):
    y = lax.axis_index("y")
    out[y] = own[...]
    out[lax.rem(y + 1, 4)] = down[...]
    out[lax.rem(y + 2, 4)] = far[...]
    out[lax.rem(y + 3, 4)] = up[...]


def plane_body(own, up, down, far_a, far_b, out):
    z = lax.axis_index("z")
    for y in range(4):
        rows = slice(y * 32, y * 32 + 32)
        out[z, rows] = own[y]
        out[lax.rem(z + 1, 4), rows] = down[y]
        out[lax.rem(z + 2, 4), rows] = (far_a if y < 2 else far_b)[y % 2]
        out[lax.rem(z + 3, 4), rows] = up[y]


def lend_body(mine, theirs, out):
    out[...] = jnp.where(lax.axis_index("core") == lax.axis_index("row"), theirs[...], mine[...])


def finish_body(mine, theirs, lent, solved):
    row = lax.axis_index("row")
    solved[row] = jnp.where(lax.axis_index("core") == row, mine[...], theirs[...])
    solved[1 - row] = lent[...]


def update_body(group, mine, theirs, rhs, *refs):
    count = len(group)
    own, other = refs[:count], refs[count : 2 * count]
    sent = refs[2 * count] if group[0] == 0 else None
    out, rhs_in, out_buf, in_sems, out_sems = refs[-5:]
    row = lax.axis_index("row")
    same = lax.axis_index("core") == row
    tiles = [(k, a) for k, size in enumerate(SIZES[g] for g in group) for a in range(0, size, TILE)]
    loads, stores = [], []
    for t, (k, a) in enumerate(tiles):
        columns = pl.ds(CUTS[group[k]] + a, TILE)
        loads.append(pltpu.make_async_copy(rhs.at[:, columns], rhs_in.at[t], in_sems.at[t]))
        stores.append(pltpu.make_async_copy(out_buf.at[t], out.at[:, columns], out_sems.at[t]))
        loads[-1].start()
    left = jnp.where(same, mine[...], theirs[...])
    right = jnp.where(same, theirs[...], mine[...])
    for t, (k, a) in enumerate(tiles):
        rows = pl.ds(a, TILE)
        arrived = other[k][rows, :]
        if group[k] == 0:
            arrived = jnp.where((column() < 2), sent[rows, :], arrived)
        first = dot_nt(left, own[k][rows, :])
        second = dot_nt(right, arrived)
        if group[k] == 0:
            drop = (column() < 2) & (row >= column())
            first = jnp.where(drop, jnp.zeros_like(first), first)
            drop = (column() < 2) & (1 - row >= column())
            second = jnp.where(drop, jnp.zeros_like(second), second)
        loads[t].wait()
        out_buf[t] = rhs_in[t] - (first + second)
        stores[t].start()
    for store in stores:
        store.wait()


def update(group, mine, theirs, rhs, own, other, sent, before):
    width = sum(SIZES[g] for g in group)
    count = width // TILE
    operands = [mine, theirs, rhs] + [own[g] for g in group] + [other[g] for g in group]
    specs = [VMEM, VMEM, HBM] + [VMEM] * (2 * len(group))
    if group[0] == 0:
        operands.append(sent)
        specs.append(VMEM)
    aliases = {}
    if before is not None:
        aliases = {len(operands): 0}
        operands.append(before)
        specs.append(HBM)
    return pl.pallas_call(
        functools.partial(update_body, group),
        in_specs=specs,
        out_specs=HBM,
        out_shape=jax.ShapeDtypeStruct(rhs.shape, F32),
        input_output_aliases=aliases,
        scratch_shapes=[
            pltpu.VMEM((count, NB, TILE), F32),
            pltpu.VMEM((count, NB, TILE), F32),
            pltpu.SemaphoreType.DMA((count,)),
            pltpu.SemaphoreType.DMA((count,)),
        ],
        compiler_params=pltpu.CompilerParams(vmem_limit_bytes=(6 << 20) + 6 * NB * width * 4),
        cost_estimate=pl.CostEstimate(
            flops=4 * NB * NB * width, bytes_accessed=4 << 20, transcendentals=0
        ),
        name="update",
    )(*operands)


def move(value, axis, pairs):
    return lax.ppermute(value, axis, pairs)


def shift(value, axis, by):
    return move(value, axis, [(i, (i + by) % 4) for i in range(4)])


def toggle(value, axis, by):
    return move(value, axis, [(i, i ^ by) for i in range(4)])


def shards(panel, rhs, diag_inverse):
    swap = [(0, 1), (1, 0)]

    own = list(call(
        cut_body, [panel], [HBM], [shape(SIZES[0], NB)],
        [pltpu.SemaphoreType.DMA(())], room=11264,
    ))
    pairs = [(c, 64 + c) for c in range(2, 64)]
    other = [
        move(own[0], ALL, pairs + [(b, a) for a, b in pairs] + [(i, i) for i in (0, 1, 64, 65)])
    ]
    sent = move(own[0], ALL, [(1, 65), (65, 1)] + [(i, i) for i in range(128) if i not in (1, 65)])
    base, low, piece = call(
        first_body, [rhs, diag_inverse, panel], [HBM] * 3,
        [shape(NB, NB, dtype=F32), shape(NB, NB), shape(SIZES[1], NB)],
        [pltpu.VMEM((NB, NB), F32), pltpu.VMEM((NB, NB), BF16), pltpu.SemaphoreType.DMA((6,))],
        6 * NB**3, 12800,
    )
    own.append(piece)
    arrived = move(low, "core", swap)
    other.append(move(own[1], "row", swap))
    made = call(
        second_body, [base, low, arrived, own[0], sent, diag_inverse, panel],
        [VMEM] * 5 + [HBM] * 2,
        [shape(NB // 4, NB)] * 4 + [shape(size, NB) for size in SIZES[2:]],
        [pltpu.VMEM((NB, NB), BF16), pltpu.SemaphoreType.DMA((len(SIZES),))],
        8 * NB**3, 18432,
    )
    quarters, own = made[:4], own + list(made[4:])

    got = [toggle(quarters[q], "z", q) for q in range(1, 4)]
    parts = call(
        functools.partial(choose_body, "z"), [quarters[0]] + got, [VMEM] * 4,
        [shape(32, NB)] * 4,
    )
    got = [toggle(parts[q], "y", q) for q in range(1, 4)]
    (mine,) = call(
        functools.partial(choose_body, "y"), [parts[0]] + got, [VMEM] * 4,
        [shape(32, NB)],
    )
    along = move(mine, "xh", swap)
    for k in range(2, len(SIZES)):
        other.append(move(own[k], "row", swap))
    (mine,) = call(select_body, [mine, along], [VMEM] * 2, [shape(32, NB)])
    up, down, far = (shift(mine, "y", by) for by in (1, -1, 2))
    (line,) = call(ring_body, [mine, up, down, far], [VMEM] * 4, [shape(4, 32, NB)])
    up, down = shift(line, "z", 1), shift(line, "z", -1)
    far_a, far_b = shift(up[:2], "z", 1), shift(down[2:], "z", -1)
    (plane,) = call(
        plane_body, [line, up, down, far_a, far_b], [VMEM] * 5,
        [shape(4, 128, NB)],
    )
    mine = plane.reshape(NB, NB)
    theirs = move(mine, "core", swap)
    (lent,) = call(lend_body, [mine, theirs], [VMEM] * 2, [shape(NB, NB)])
    lent = move(lent, ("row", "xh"), [(0, 3), (3, 0), (1, 2), (2, 1)])
    updated = None
    for group in GROUPS:
        updated = update(group, mine, theirs, rhs, own, other, sent, updated)
    (solved,) = call(finish_body, [mine, theirs, lent], [VMEM] * 3, [shape(2, NB, NB)])
    return solved.reshape(2 * NB, NB), updated


def solution(mesh):
    split = Mesh(mesh.devices.reshape(2, 4, 4, 2, 2), ALL)
    return jax.shard_map(
        shards,
        mesh=split,
        in_specs=(P(COL, "row"), P("row", COL), P()),
        out_specs=(P(None, "row"), P("row", COL)),
        check_vma=False,
    )
```

time: 1040 us -> 120 us (0.12)
  the two profiles are of different devices: /device:TPU:1 before, /device:TPU:4 now
where the time goes in v2:
time: 120 us; the launch traced here: 119 us
  waiting for transfers between devices  73.2 us (61%)
  starting transfers between devices  28.5 us (24%)
  Pallas kernels  16.9 us (14%)
    ppermute x24, waiting for transfers between devices, move(): return lax.ppermute(value, axis, pairs)  73.2 us
    ppermute x24, starting transfers between devices, move(): return lax.ppermute(value, axis, pairs)  28.5 us
    pallas_call x4, Pallas kernels, update(): pl.pallas_call(functools.partial(update_body, group), in_specs=specs, out...  11.6 us
    pallas_call x10, Pallas kernels, call(): pl.pallas_call(body, in_specs=in_specs, out_specs=[VMEM] * len(outs), out...  5.32 us
  transfers between devices with their start and end apart: 24, of which 16 were waited for; matrix products, arithmetic and copies ran while one was open for 0% of the time, Pallas kernels for 11%

profile of v2, /device:TPU:4, one launch (start us, length us, event | category | flops | bytes accessed | tf_op | source)
XLA Modules:
  0.0 119.5 jit_solution(4079923339694799198)
XLA Ops:
  0.6 1.1 shard_map.51.block.refs_0_
  2.5 1.4 %shard_map.50 = (f32[512,512]{1,0:T(8,128)S(1)}, bf16[512,512]{1,0:T(8,128)(2,1)S(1)}, bf16[768,512]{1,0:T(8,128)(2,1)S(1)}) custom-call(f32[512,3072]{1,0:T(8,128)} %rhs.9, bf16[2,512,512]{2,1,0:T(8,128)(2,1)} %inv.3, bf16[3072,512]{1,0:T(8,128)(2,1)} %panel.5), custom_call_target="tpu_custom_call" | custom-call | flops 805306368 | bytes 1048576 | tf_op jit(solution)/shard_map/pallas_call | solution.py:51
  4.0 1.9 %collective-permute-done.arrived = bf16[512,512]{1,0:T(8,128)(2,1)S(1)} collective-permute-done((bf16[512,512]{1,0:T(8,128)(2,1)S(1)}, bf16[512,512]{1,0:T(8,128)(2,1)S(1)}, u32[]{:S(2)}, u32[]{:S(2)}) %collective-permute-start) | collective-permute-done | bytes 524320 | tf_op jit(solution)/shard_map/ppermute | solution.py:241
  5.9 1.6 %shard_map.52 = (bf16[128,512]{1,0:T(8,128)(2,1)S(1)}, bf16[128,512]{1,0:T(8,128)(2,1)S(1)}, bf16[128,512]{1,0:T(8,128)(2,1)S(1)}, bf16[128,512]{1,0:T(8,128)(2,...) custom-call(f32[512,512]{1,0:T(8,128)S(1)} %get-tuple-element.17.bas, ...), custom_call_target="tpu_custom_call" | custom-call | flops 1073741824 | bytes 1048576 | tf_op jit(solution)/shard_map/pallas_call | solution.py:51
  7.5 2.0 %collective-permute-start.2 = (bf16[128,512]{1,0:T(8,128)(2,1)S(1)}, bf16[128,512]{1,0:T(8,128)(2,1)S(1)}, u32[]{:S(2)}, u32[]{:S(2)}) collective-permute-start(bf16[128,512]{1,0:T(8,128)(2,1)S(1)} %get-tuple-element.20), channel_id=1, source_target_pairs={{0,16},{16,0},{32,48},{48,32},{1,17},{17,1},{33,49},{49,33},{2,18}... | collective-permute-start | bytes 393224 | tf_op jit(solution)/shard_map/ppermute | solution.py:241
  9.5 3.6 %collective-permute-start.3 = (bf16[128,512]{1,0:T(8,128)(2,1)S(1)}, bf16[128,512]{1,0:T(8,128)(2,1)S(1)}, u32[]{:S(2)}, u32[]{:S(2)}) collective-permute-start(bf16[128,512]{1,0:T(8,128)(2,1)S(1)} %get-tuple-element.21), channel_id=1, source_target_pairs={{0,32},{16,48},{32,0},{48,16},{1,33},{17,49},{33,1},{49,17},{2,34}... | collective-permute-start | bytes 393224 | tf_op jit(solution)/shard_map/ppermute | solution.py:241
  13.3 6.2 %collective-permute-done.3.refs_2_ = bf16[128,512]{1,0:T(8,128)(2,1)S(1)} collective-permute-done((bf16[128,512]{1,0:T(8,128)(2,1)S(1)}, bf16[128,512]{1,0:T(8,128)(2,1)S(1)}, u32[]{:S(2)}, u32[]{:S(2)}) %collective-permute-start.3) | collective-permute-done | bytes 131104 | tf_op jit(solution)/shard_map/ppermute | solution.py:241
  19.5 2.2 %collective-permute-done.4.refs_3_ = bf16[128,512]{1,0:T(8,128)(2,1)S(1)} collective-permute-done((bf16[128,512]{1,0:T(8,128)(2,1)S(1)}, bf16[128,512]{1,0:T(8,128)(2,1)S(1)}, u32[]{:S(2)}, u32[]{:S(2)}) %collective-permute-start.4) | collective-permute-done | bytes 131104 | tf_op jit(solution)/shard_map/ppermute | solution.py:241
  21.7 1.7 %collective-permute-start.5 = (bf16[32,512]{1,0:T(8,128)(2,1)S(1)}, bf16[32,512]{1,0:T(8,128)(2,1)S(1)}, u32[]{:S(2)}, u32[]{:S(2)}) collective-permute-start(bf16[32,512]{1,0:T(8,128)(2,1)S(1)} %get-tuple-element.24), channel_id=1, source_target_pairs={{0,4},{4,0},{8,12},{12,8},{1,5},{5,1},{9,13},{13,9},{2,6},{6,2},{1... | collective-permute-start | bytes 98312 | tf_op jit(solution)/shard_map/ppermute | solution.py:241
  23.4 2.9 %collective-permute-start.6 = (bf16[32,512]{1,0:T(8,128)(2,1)S(1)}, bf16[32,512]{1,0:T(8,128)(2,1)S(1)}, u32[]{:S(2)}, u32[]{:S(2)}) collective-permute-start(bf16[32,512]{1,0:T(8,128)(2,1)S(1)} %get-tuple-element.25), channel_id=1, source_target_pairs={{0,8},{4,12},{8,0},{12,4},{1,9},{5,13},{9,1},{13,5},{2,10},{6,14},... | collective-permute-start | bytes 98312 | tf_op jit(solution)/shard_map/ppermute | solution.py:241
  26.5 2.3 %collective-permute-done.6.refs_2_ = bf16[32,512]{1,0:T(8,128)(2,1)S(1)} collective-permute-done((bf16[32,512]{1,0:T(8,128)(2,1)S(1)}, bf16[32,512]{1,0:T(8,128)(2,1)S(1)}, u32[]{:S(2)}, u32[]{:S(2)}) %collective-permute-start.6) | collective-permute-done | bytes 32800 | tf_op jit(solution)/shard_map/ppermute | solution.py:241
  28.8 2.6 %collective-permute-done.7.refs_3_ = bf16[32,512]{1,0:T(8,128)(2,1)S(1)} collective-permute-done((bf16[32,512]{1,0:T(8,128)(2,1)S(1)}, bf16[32,512]{1,0:T(8,128)(2,1)S(1)}, u32[]{:S(2)}, u32[]{:S(2)}) %collective-permute-start.7) | collective-permute-done | bytes 32800 | tf_op jit(solution)/shard_map/ppermute | solution.py:241
  31.9 4.9 %collective-permute-done.8.far = bf16[32,512]{1,0:T(8,128)(2,1)S(1)} collective-permute-done((bf16[32,512]{1,0:T(8,128)(2,1)S(1)}, bf16[32,512]{1,0:T(8,128)(2,1)S(1)}, u32[]{:S(2)}, u32[]{:S(2)}) %collective-permute-start.8) | collective-permute-done | bytes 32800 | tf_op jit(solution)/shard_map/ppermute | solution.py:241
  37.9 1.0 collective-permute-start.9
  38.9 1.9 %collective-permute-done.10.down = bf16[32,512]{1,0:T(8,128)(2,1)S(1)} collective-permute-done((bf16[32,512]{1,0:T(8,128)(2,1)S(1)}, bf16[32,512]{1,0:T(8,128)(2,1)S(1)}, u32[]{:S(2)}, u32[]{:S(2)}) %collective-permute-start.10) | collective-permute-done | bytes 32800 | tf_op jit(solution)/shard_map/ppermute | solution.py:241
  40.8 1.7 %collective-permute-done.11.far = bf16[32,512]{1,0:T(8,128)(2,1)S(1)} collective-permute-done((bf16[32,512]{1,0:T(8,128)(2,1)S(1)}, bf16[32,512]{1,0:T(8,128)(2,1)S(1)}, u32[]{:S(2)}, u32[]{:S(2)}) %collective-permute-start.11) | collective-permute-done | bytes 32800 | tf_op jit(solution)/shard_map/ppermute | solution.py:241
  42.5 0.9 collective-permute-done.9.up
  43.6 3.2 %collective-permute-start.13 = (bf16[4,32,512]{2,1,0:T(8,128)(2,1)S(1)}, bf16[4,32,512]{2,1,0:T(8,128)(2,1)S(1)}, u32[]{:S(2)}, u32[]{:S(2)}) collective-permute-start(bf16[4,32,512]{2,1,0:T(8,128)(2,1)S(1)} %shard_map.56.own), channel_id=1, source_target_pairs={{0,48},{16,0},{32,16},{48,32},{1,49},{17,1},{33,17},{49,33},{2,50}... | collective-permute-start | bytes 393224 | tf_op jit(solution)/shard_map/ppermute | solution.py:241
  46.8 3.0 %collective-permute-done.12.up = bf16[4,32,512]{2,1,0:T(8,128)(2,1)S(1)} collective-permute-done((bf16[4,32,512]{2,1,0:T(8,128)(2,1)S(1)}, bf16[4,32,512]{2,1,0:T(8,128)(2,1)S(1)}, u32[]{:S(2)}, u32[]{:S(2)}) %collective-permute-start.12) | collective-permute-done | bytes 131104 | tf_op jit(solution)/shard_map/ppermute | solution.py:241
  49.8 3.3 %collective-permute-start.15 = (bf16[2,32,512]{2,1,0:T(8,128)(2,1)S(1)}, bf16[2,32,512]{2,1,0:T(8,128)(2,1)S(1)}, u32[]{:S(2)}, u32[]{:S(2)}) collective-permute-start(bf16[2,32,512]{2,1,0:T(8,128)(2,1)S(1)} %slice.9), channel_id=1, source_target_pairs={{0,48},{16,0},{32,16},{48,32},{1,49},{17,1},{33,17},{49,33},{2,50}... | collective-permute-start | bytes 196616 | tf_op jit(solution)/shard_map/ppermute | solution.py:241
  53.1 1.2 %collective-permute-start.22 = (bf16[768,512]{1,0:T(8,128)(2,1)S(1)}, bf16[768,512]{1,0:T(8,128)(2,1)S(1)}, u32[]{:S(2)}, u32[]{:S(2)}) collective-permute-start(bf16[768,512]{1,0:T(8,128)(2,1)S(1)} %get-tuple-element.30.refs_1_), channel_id=1, source_target_pairs={{0,64},{64,0},{1,65},{65,1},{2,66},{66,2},{3,67},{67,3},{4,68},{68... | collective-permute-start | bytes 2359304 | tf_op jit(solution)/shard_map/ppermute | solution.py:241
  55.4 3.1 %collective-permute-start.21 = (bf16[512,512]{1,0:T(8,128)(2,1)S(1)}, bf16[512,512]{1,0:T(8,128)(2,1)S(1)}, u32[]{:S(2)}, u32[]{:S(2)}) collective-permute-start(bf16[512,512]{1,0:T(8,128)(2,1)S(1)} %shard_map.51.block.refs_0_), channel_id=1, source_target_pairs={{2,66},{3,67},{4,68},{5,69},{6,70},{7,71},{8,72},{9,73},{10,74},{1... | collective-permute-start | bytes 1572872 | tf_op jit(solution)/shard_map/ppermute | solution.py:241
  58.5 0.9 collective-permute-start.20
  59.5 42.0 %collective-permute-done.21.refs_3_ = bf16[512,512]{1,0:T(8,128)(2,1)S(1)} collective-permute-done((bf16[512,512]{1,0:T(8,128)(2,1)S(1)}, bf16[512,512]{1,0:T(8,128)(2,1)S(1)}, u32[]{:S(2)}, u32[]{:S(2)}) %collective-permute-start.21) | collective-permute-done | bytes 524320 | tf_op jit(solution)/shard_map/ppermute | solution.py:241
  101.6 1.2 %collective-permute-start.19 = (bf16[256,512]{1,0:T(8,128)(2,1)S(1)}, bf16[256,512]{1,0:T(8,128)(2,1)S(1)}, u32[]{:S(2)}, u32[]{:S(2)}) collective-permute-start(bf16[256,512]{1,0:T(8,128)(2,1)S(1)} %get-tuple-element.28.refs_0_), channel_id=1, source_target_pairs={{0,64},{64,0},{1,65},{65,1},{2,66},{66,2},{3,67},{67,3},{4,68},{68... | collective-permute-start | bytes 786440 | tf_op jit(solution)/shard_map/ppermute | solution.py:241
  103.6 5.7 %update.4.refs_2_ = f32[512,3072]{1,0:T(8,128)} custom-call(bf16[512,512]{1,0:T(8,128)(2,1)S(1)} %bitcast.6, bf16[512,512]{1,0:T(8,128)(2,1)S(1)} %collective-permute-done.16.theirs, f32[512,3072]{1,0:T(8,128)S(1)} %bitcast.3, bf16[512,512]{1,0:T(8,128)(2,1)S(1)} %shard_map.51.block.refs_0_, bf16[768,512]{1,0:T(8,128)(2,1)S(1)} %get-tuple-element.30.refs_1_, ...), custom_call_target="tpu_custom_call" | custom-call | flops 2147483648 | bytes 4194304 | tf_op jit(solution)/shard_map/update/pallas_call | solution.py:220
  109.3 1.6 %collective-permute-done.20.refs_1_ = bf16[512,512]{1,0:T(8,128)(2,1)S(1)} collective-permute-done((bf16[512,512]{1,0:T(8,128)(2,1)S(1)}, bf16[512,512]{1,0:T(8,128)(2,1)S(1)}, u32[]{:S(2)}, u32[]{:S(2)}) %collective-permute-start.20) | collective-permute-done | bytes 524320 | tf_op jit(solution)/shard_map/ppermute | solution.py:241
  111.0 2.2 %update.5.refs_2_ = f32[512,3072]{1,0:T(8,128)} custom-call(bf16[512,512]{1,0:T(8,128)(2,1)S(1)} %bitcast.7, bf16[512,512]{1,0:T(8,128)(2,1)S(1)} %collective-permute-done.16.theirs, f32[512,3072]{1,0:T(8,128)S(1)} %bitcast.3, bf16[512,512]{1,0:T(8,128)(2,1)S(1)} %get-tuple-element.29.refs_0_, ...), custom_call_target="tpu_custom_call", output_to_operand_aliasing={{}: (5, {})} | custom-call | flops 536870912 | bytes 4194304 | tf_op jit(solution)/shard_map/update/pallas_call | solution.py:220
  113.8 1.8 %update.6.refs_2_ = f32[512,3072]{1,0:T(8,128)} custom-call(bf16[512,512]{1,0:T(8,128)(2,1)S(1)} %bitcast.8, bf16[512,512]{1,0:T(8,128)(2,1)S(1)} %collective-permute-done.16.theirs, f32[512,3072]{1,0:T(8,128)S(1)} %bitcast.3, bf16[256,512]{1,0:T(8,128)(2,1)S(1)} %get-tuple-element.28.refs_0_, ...), custom_call_target="tpu_custom_call", output_to_operand_aliasing={{}: (5, {})} | custom-call | flops 268435456 | bytes 4194304 | tf_op jit(solution)/shard_map/update/pallas_call | solution.py:220
  115.6 1.0 collective-permute-done.18.refs_1_
  116.6 1.8 %update.7 = f32[512,3072]{1,0:T(8,128)} custom-call(bf16[512,512]{1,0:T(8,128)(2,1)S(1)} %bitcast.9, bf16[512,512]{1,0:T(8,128)(2,1)S(1)} %collective-permute-done.16.theirs, f32[512,3072]{1,0:T(8,128)S(1)} %bitcast.3, bf16[256,512]{1,0:T(8,128)(2,1)S(1)} %get-tuple-element.27.refs_0_, ...), custom_call_target="tpu_custom_call", output_to_operand_aliasing={{}: (5, {})} | custom-call | flops 268435456 | bytes 4194304 | tf_op jit(solution)/shard_map/update/pallas_call | solution.py:220
  118.4 1.1 shard_map.59
  (39 shorter events, 5.5 us)
Async XLA Ops:
  0.6 5.2 %copy-start = (bf16[2,512,512]{2,1,0:T(8,128)(2,1)S(1)}, bf16[2,512,512]{2,1,0:T(8,128)(2,1)}, u32[]{:S(2)}) copy-start(bf16[2,512,512]{2,1,0:T(8,128)(2,1)} %inv.3) | copy-start | bytes 3145732
  1.8 2.2 %collective-permute-start.1 = (bf16[512,512]{1,0:T(8,128)(2,1)S(1)}, bf16[512,512]{1,0:T(8,128)(2,1)S(1)}, u32[]{:S(2)}, u32[]{:S(2)}) collective-permute-start(bf16[512,512]{1,0:T(8,128)(2,1)S(1)} %shard_map.51.block.refs_0_), channel_id=1, source_target_pairs={{1,65},{65,1},{0,0},{2,2},{3,3},{4,4},{5,5},{6,6},{7,7},{8,8},{9,9... | collective-permute-start | bytes 1572872 | tf_op jit(solution)/shard_map/ppermute | solution.py:241
  2.5 101.1 %slice-start = ((s8[6291456]{0:T(1024)(128)(4,1)}), s8[2097152]{0:T(1024)(128)(4,1)S(1)}, s32[]{:S(2)}) async-start(s8[6291456]{0:T(1024)(128)(4,1)} %bitcast.2), calls=%async_computation | async-start | bytes 4194304
  3.9 2.0 %collective-permute-start = (bf16[512,512]{1,0:T(8,128)(2,1)S(1)}, bf16[512,512]{1,0:T(8,128)(2,1)S(1)}, u32[]{:S(2)}, u32[]{:S(2)}) collective-permute-start(bf16[512,512]{1,0:T(8,128)(2,1)S(1)} %get-tuple-element.18.low), channel_id=1, source_target_pairs={{0,1},{1,0},{2,3},{3,2},{4,5},{5,4},{6,7},{7,6},{8,9},{9,8},{10,11... | collective-permute-start | bytes 1572872 | tf_op jit(solution)/shard_map/ppermute | solution.py:241
  5.9 97.7 %slice-start.1 = ((s8[6291456]{0:T(1024)(128)(4,1)}), s8[4194304]{0:T(1024)(128)(4,1)S(1)}, s32[]{:S(2)}) async-start(s8[6291456]{0:T(1024)(128)(4,1)} %bitcast.2), calls=%async_computation.1 | async-start | bytes 8388608
  7.5 5.8 %collective-permute-start.2 = (bf16[128,512]{1,0:T(8,128)(2,1)S(1)}, bf16[128,512]{1,0:T(8,128)(2,1)S(1)}, u32[]{:S(2)}, u32[]{:S(2)}) collective-permute-start(bf16[128,512]{1,0:T(8,128)(2,1)S(1)} %get-tuple-element.20), channel_id=1, source_target_pairs={{0,16},{16,0},{32,48},{48,32},{1,17},{17,1},{33,49},{49,33},{2,18}... | collective-permute-start | bytes 393224 | tf_op jit(solution)/shard_map/ppermute | solution.py:241
  9.5 10.0 %collective-permute-start.3 = (bf16[128,512]{1,0:T(8,128)(2,1)S(1)}, bf16[128,512]{1,0:T(8,128)(2,1)S(1)}, u32[]{:S(2)}, u32[]{:S(2)}) collective-permute-start(bf16[128,512]{1,0:T(8,128)(2,1)S(1)} %get-tuple-element.21), channel_id=1, source_target_pairs={{0,32},{16,48},{32,0},{48,16},{1,33},{17,49},{33,1},{49,17},{2,34}... | collective-permute-start | bytes 393224 | tf_op jit(solution)/shard_map/ppermute | solution.py:241
  13.1 8.6 %collective-permute-start.4 = (bf16[128,512]{1,0:T(8,128)(2,1)S(1)}, bf16[128,512]{1,0:T(8,128)(2,1)S(1)}, u32[]{:S(2)}, u32[]{:S(2)}) collective-permute-start(bf16[128,512]{1,0:T(8,128)(2,1)S(1)} %get-tuple-element.22), channel_id=1, source_target_pairs={{0,48},{16,32},{32,16},{48,0},{1,49},{17,33},{33,17},{49,1},{2,50}... | collective-permute-start | bytes 393224 | tf_op jit(solution)/shard_map/ppermute | solution.py:241
  21.7 4.8 %collective-permute-start.5 = (bf16[32,512]{1,0:T(8,128)(2,1)S(1)}, bf16[32,512]{1,0:T(8,128)(2,1)S(1)}, u32[]{:S(2)}, u32[]{:S(2)}) collective-permute-start(bf16[32,512]{1,0:T(8,128)(2,1)S(1)} %get-tuple-element.24), channel_id=1, source_target_pairs={{0,4},{4,0},{8,12},{12,8},{1,5},{5,1},{9,13},{13,9},{2,6},{6,2},{1... | collective-permute-start | bytes 98312 | tf_op jit(solution)/shard_map/ppermute | solution.py:241
  23.4 5.4 %collective-permute-start.6 = (bf16[32,512]{1,0:T(8,128)(2,1)S(1)}, bf16[32,512]{1,0:T(8,128)(2,1)S(1)}, u32[]{:S(2)}, u32[]{:S(2)}) collective-permute-start(bf16[32,512]{1,0:T(8,128)(2,1)S(1)} %get-tuple-element.25), channel_id=1, source_target_pairs={{0,8},{4,12},{8,0},{12,4},{1,9},{5,13},{9,1},{13,5},{2,10},{6,14},... | collective-permute-start | bytes 98312 | tf_op jit(solution)/shard_map/ppermute | solution.py:241
  26.3 5.1 %collective-permute-start.7 = (bf16[32,512]{1,0:T(8,128)(2,1)S(1)}, bf16[32,512]{1,0:T(8,128)(2,1)S(1)}, u32[]{:S(2)}, u32[]{:S(2)}) collective-permute-start(bf16[32,512]{1,0:T(8,128)(2,1)S(1)} %get-tuple-element.26), channel_id=1, source_target_pairs={{0,12},{4,8},{8,4},{12,0},{1,13},{5,9},{9,5},{13,1},{2,14},{6,10},... | collective-permute-start | bytes 98312 | tf_op jit(solution)/shard_map/ppermute | solution.py:241
  31.4 5.4 %collective-permute-start.8 = (bf16[32,512]{1,0:T(8,128)(2,1)S(1)}, bf16[32,512]{1,0:T(8,128)(2,1)S(1)}, u32[]{:S(2)}, u32[]{:S(2)}) collective-permute-start(bf16[32,512]{1,0:T(8,128)(2,1)S(1)} %shard_map.54.near), channel_id=1, source_target_pairs={{0,2},{2,0},{1,3},{3,1},{4,6},{6,4},{5,7},{7,5},{8,10},{10,8},{9,1... | collective-permute-start | bytes 98312 | tf_op jit(solution)/shard_map/ppermute | solution.py:241
  36.9 3.9 %collective-permute-start.10 = (bf16[32,512]{1,0:T(8,128)(2,1)S(1)}, bf16[32,512]{1,0:T(8,128)(2,1)S(1)}, u32[]{:S(2)}, u32[]{:S(2)}) collective-permute-start(bf16[32,512]{1,0:T(8,128)(2,1)S(1)} %shard_map.55.own), channel_id=1, source_target_pairs={{0,12},{4,0},{8,4},{12,8},{1,13},{5,1},{9,5},{13,9},{2,14},{6,2},{... | collective-permute-start | bytes 98312 | tf_op jit(solution)/shard_map/ppermute | solution.py:241
  37.1 5.4 %collective-permute-start.11 = (bf16[32,512]{1,0:T(8,128)(2,1)S(1)}, bf16[32,512]{1,0:T(8,128)(2,1)S(1)}, u32[]{:S(2)}, u32[]{:S(2)}) collective-permute-start(bf16[32,512]{1,0:T(8,128)(2,1)S(1)} %shard_map.55.own), channel_id=1, source_target_pairs={{0,8},{4,12},{8,0},{12,4},{1,9},{5,13},{9,1},{13,5},{2,10},{6,14},... | collective-permute-start | bytes 98312 | tf_op jit(solution)/shard_map/ppermute | solution.py:241
  37.9 5.6 %collective-permute-start.9 = (bf16[32,512]{1,0:T(8,128)(2,1)S(1)}, bf16[32,512]{1,0:T(8,128)(2,1)S(1)}, u32[]{:S(2)}, u32[]{:S(2)}) collective-permute-start(bf16[32,512]{1,0:T(8,128)(2,1)S(1)} %shard_map.55.own), channel_id=1, source_target_pairs={{0,4},{4,8},{8,12},{12,0},{1,5},{5,9},{9,13},{13,1},{2,6},{6,10},{... | collective-permute-start | bytes 98312 | tf_op jit(solution)/shard_map/ppermute | solution.py:241
  43.5 6.3 %collective-permute-start.12 = (bf16[4,32,512]{2,1,0:T(8,128)(2,1)S(1)}, bf16[4,32,512]{2,1,0:T(8,128)(2,1)S(1)}, u32[]{:S(2)}, u32[]{:S(2)}) collective-permute-start(bf16[4,32,512]{2,1,0:T(8,128)(2,1)S(1)} %shard_map.56.own), channel_id=1, source_target_pairs={{0,16},{16,32},{32,48},{48,0},{1,17},{17,33},{33,49},{49,1},{2,18}... | collective-permute-start | bytes 393224 | tf_op jit(solution)/shard_map/ppermute | solution.py:241
  43.6 6.2 %collective-permute-start.13 = (bf16[4,32,512]{2,1,0:T(8,128)(2,1)S(1)}, bf16[4,32,512]{2,1,0:T(8,128)(2,1)S(1)}, u32[]{:S(2)}, u32[]{:S(2)}) collective-permute-start(bf16[4,32,512]{2,1,0:T(8,128)(2,1)S(1)} %shard_map.56.own), channel_id=1, source_target_pairs={{0,48},{16,0},{32,16},{48,32},{1,49},{17,1},{33,17},{49,33},{2,50}... | collective-permute-start | bytes 393224 | tf_op jit(solution)/shard_map/ppermute | solution.py:241
  49.7 5.5 %collective-permute-start.14 = (bf16[2,32,512]{2,1,0:T(8,128)(2,1)S(1)}, bf16[2,32,512]{2,1,0:T(8,128)(2,1)S(1)}, u32[]{:S(2)}, u32[]{:S(2)}) collective-permute-start(bf16[2,32,512]{2,1,0:T(8,128)(2,1)S(1)} %slice.8), channel_id=1, source_target_pairs={{0,16},{16,32},{32,48},{48,0},{1,17},{17,33},{33,49},{49,1},{2,18}... | collective-permute-start | bytes 196616 | tf_op jit(solution)/shard_map/ppermute | solution.py:241
  49.8 5.4 %collective-permute-start.15 = (bf16[2,32,512]{2,1,0:T(8,128)(2,1)S(1)}, bf16[2,32,512]{2,1,0:T(8,128)(2,1)S(1)}, u32[]{:S(2)}, u32[]{:S(2)}) collective-permute-start(bf16[2,32,512]{2,1,0:T(8,128)(2,1)S(1)} %slice.9), channel_id=1, source_target_pairs={{0,48},{16,0},{32,16},{48,32},{1,49},{17,1},{33,17},{49,33},{2,50}... | collective-permute-start | bytes 196616 | tf_op jit(solution)/shard_map/ppermute | solution.py:241
  53.1 49.7 %collective-permute-start.22 = (bf16[768,512]{1,0:T(8,128)(2,1)S(1)}, bf16[768,512]{1,0:T(8,128)(2,1)S(1)}, u32[]{:S(2)}, u32[]{:S(2)}) collective-permute-start(bf16[768,512]{1,0:T(8,128)(2,1)S(1)} %get-tuple-element.30.refs_1_), channel_id=1, source_target_pairs={{0,64},{64,0},{1,65},{65,1},{2,66},{66,2},{3,67},{67,3},{4,68},{68... | collective-permute-start | bytes 2359304 | tf_op jit(solution)/shard_map/ppermute | solution.py:241
  54.3 49.3 %collective-permute-start.23 = (bf16[768,512]{1,0:T(8,128)(2,1)S(1)}, bf16[768,512]{1,0:T(8,128)(2,1)S(1)}, u32[]{:S(2)}, u32[]{:S(2)}) collective-permute-start(bf16[768,512]{1,0:T(8,128)(2,1)S(1)} %get-tuple-element.31.refs_2_), channel_id=1, source_target_pairs={{0,64},{64,0},{1,65},{65,1},{2,66},{66,2},{3,67},{67,3},{4,68},{68... | collective-permute-start | bytes 2359304 | tf_op jit(solution)/shard_map/ppermute | solution.py:241
  55.3 4.1 %collective-permute-start.16 = (bf16[512,512]{1,0:T(8,128)(2,1)S(1)}, bf16[512,512]{1,0:T(8,128)(2,1)S(1)}, u32[]{:S(2)}, u32[]{:S(2)}) collective-permute-start(bf16[512,512]{1,0:T(8,128)(2,1)S(1)} %bitcast.4), channel_id=1, source_target_pairs={{0,1},{1,0},{2,3},{3,2},{4,5},{5,4},{6,7},{7,6},{8,9},{9,8},{10,11... | collective-permute-start | bytes 1572872 | tf_op jit(solution)/shard_map/ppermute | solution.py:241
  55.4 46.2 %collective-permute-start.21 = (bf16[512,512]{1,0:T(8,128)(2,1)S(1)}, bf16[512,512]{1,0:T(8,128)(2,1)S(1)}, u32[]{:S(2)}, u32[]{:S(2)}) collective-permute-start(bf16[512,512]{1,0:T(8,128)(2,1)S(1)} %shard_map.51.block.refs_0_), channel_id=1, source_target_pairs={{2,66},{3,67},{4,68},{5,69},{6,70},{7,71},{8,72},{9,73},{10,74},{1... | collective-permute-start | bytes 1572872 | tf_op jit(solution)/shard_map/ppermute | solution.py:241
  58.5 52.5 %collective-permute-start.20 = (bf16[512,512]{1,0:T(8,128)(2,1)S(1)}, bf16[512,512]{1,0:T(8,128)(2,1)S(1)}, u32[]{:S(2)}, u32[]{:S(2)}) collective-permute-start(bf16[512,512]{1,0:T(8,128)(2,1)S(1)} %get-tuple-element.29.refs_0_), channel_id=1, source_target_pairs={{0,64},{64,0},{1,65},{65,1},{2,66},{66,2},{3,67},{67,3},{4,68},{68... | collective-permute-start | bytes 1572872 | tf_op jit(solution)/shard_map/ppermute | solution.py:241
  59.4 59.0 %collective-permute-start.17 = (bf16[512,512]{1,0:T(8,128)(2,1)S(1)}, bf16[512,512]{1,0:T(8,128)(2,1)S(1)}, u32[]{:S(2)}, u32[]{:S(2)}) collective-permute-start(bf16[512,512]{1,0:T(8,128)(2,1)S(1)} %shard_map.58), channel_id=1, source_target_pairs={{0,66},{66,0},{2,64},{64,2},{1,67},{67,1},{3,65},{65,3},{4,70},{70... | collective-permute-start | bytes 1572872 | tf_op jit(solution)/shard_map/ppermute | solution.py:241
  101.6 12.2 %collective-permute-start.19 = (bf16[256,512]{1,0:T(8,128)(2,1)S(1)}, bf16[256,512]{1,0:T(8,128)(2,1)S(1)}, u32[]{:S(2)}, u32[]{:S(2)}) collective-permute-start(bf16[256,512]{1,0:T(8,128)(2,1)S(1)} %get-tuple-element.28.refs_0_), channel_id=1, source_target_pairs={{0,64},{64,0},{1,65},{65,1},{2,66},{66,2},{3,67},{67,3},{4,68},{68... | collective-permute-start | bytes 786440 | tf_op jit(solution)/shard_map/ppermute | solution.py:241
  102.8 13.8 %collective-permute-start.18 = (bf16[256,512]{1,0:T(8,128)(2,1)S(1)}, bf16[256,512]{1,0:T(8,128)(2,1)S(1)}, u32[]{:S(2)}, u32[]{:S(2)}) collective-permute-start(bf16[256,512]{1,0:T(8,128)(2,1)S(1)} %get-tuple-element.27.refs_0_), channel_id=1, source_target_pairs={{0,64},{64,0},{1,65},{65,1},{2,66},{66,2},{3,67},{67,3},{4,68},{68... | collective-permute-start | bytes 786440 | tf_op jit(solution)/shard_map/ppermute | solution.py:241
